TPU v7x, 256 devices: a whole 4x4x8 slice. The times are simulated.
256 devices in a mesh: dp: 8 (over x_lo, y), mp: 32 (over z, x_hi, core).
Axes of the slice: x: 4 (x_hi: 2, x_lo: 2; x = x_hi * 2 + x_lo), y: 4, z: 8, core: 2. Of those that a mesh axis runs over, the one named last changes fastest.
Arguments:
- tokens: bfloat16 [1024, 6144], P(('dp', 'mp')), may hold values from -6 to 6
- norm_gain: float32 [6144], replicated, may hold values from 0.5 to 1.5
- w_query: bfloat16 [6144, 4096], P('dp', 'mp'), as said below
- w_key: bfloat16 [6144, 4096], P('dp', 'mp'), as said below
- w_value: bfloat16 [6144, 4096], P('dp', 'mp'), may hold values from -0.078125 to 0.078125
- w_inner: bfloat16 [6144, 24576], P('dp', 'mp'), may hold values from -0.078125 to 0.078125
- bias_inner: float32 [24576], P('mp'), may hold values from -3 to 3
- w_attn_out: bfloat16 [4096, 6144], P('mp', 'dp'), may hold values from -0.09375 to 0.09375
- w_outer: bfloat16 [24576, 6144], P('mp', 'dp'), may hold values from -0.0390625 to 0.0390625
- temper: float32 [32], P('mp'), may hold values from 0.5 to 24
Outputs:
- result: bfloat16 [1024, 6144], P(('dp', 'mp'))
Inputs may be any that keep to these rules, and one draw needn't show every extreme that they name: `w_query`: entries of order 6144 ** -0.5. `w_key`: entries of order 6144 ** -0.5.
All inputs are finite; a program needn't handle non-finite values.
Results may differ from a plain program's by a relative error of at most 0.023.
Values may be sent and summed in bfloat16 or wider, within the bound.
A program may use at most 64 MiB of HBM per device.

v0:
```python
import functools
import math

import jax
import jax.numpy as jnp
from jax import lax
from jax.experimental import pallas as pl
from jax.experimental.pallas import tpu as pltpu
from jax.sharding import PartitionSpec as P

HEAD = 128
MESH = pl.DeviceIdType.MESH
F32, BF16 = jnp.float32, jnp.bfloat16


def normalize(values):
    center = values - jnp.mean(values, axis=-1, keepdims=True)
    spread = jnp.mean(center * center, axis=-1, keepdims=True)
    return center * lax.rsqrt(spread + 1e-06)


def wait_bytes(ref, sem):
    pltpu.make_async_copy(ref, ref, sem).wait()


def block_kernel(
    n_dp, n_mp,
    tokens, gain, bias, temper, w_query, w_key, w_value, w_inner, w_attn, w_outer,
    out,
    w_in, w_out, nsend, nrecv, stage, x, psend, precv, ag, acc, xsend, xrecv, dsend, drecv,
    win_sem, wout_sem, a_send, a_recv, f_send, f_recv, p_send, p_recv, g_send, g_recv,
    x_send, x_recv, d_send, d_recv,
):
    n_dev = n_dp * n_mp
    rows = tokens.shape[0]
    n_in, depth, wide = w_in.shape
    n_out = w_out.shape[0]
    per = psend.shape[2]
    i, j = lax.axis_index("dp"), lax.axis_index("mp")
    me = i * n_mp + j
    n_chip = n_mp // 2
    n_lane = n_dp * n_chip
    core, chip = lax.rem(j, 2), j // 2
    sibling = (i, j + 1 - 2 * core)
    lane = i * n_chip + chip

    def same_core(other):
        return (other // n_chip, 2 * lax.rem(other, n_chip) + core)

    barrier = pltpu.get_barrier_semaphore()

    def greet(d, carry):
        t = lax.rem(me + d, n_dev)
        pl.semaphore_signal(
            barrier, inc=1, device_id=(t // n_mp, lax.rem(t, n_mp)), device_id_type=MESH
        )
        return carry

    lax.fori_loop(1, n_dev, greet, 0)

    for c, w in enumerate((w_query, w_key, w_value)):
        pltpu.make_async_copy(w, w_in.at[c], win_sem.at[c]).start()
    for c in range(3, n_in):
        pltpu.make_async_copy(
            w_inner.at[:, pl.ds((c - 3) * wide, wide)], w_in.at[c], win_sem.at[c]
        ).start()
    pltpu.make_async_copy(w_attn, w_out.at[0], wout_sem.at[0]).start()
    for c in range(1, n_out):
        pltpu.make_async_copy(
            w_outer.at[pl.ds((c - 1) * wide, wide), :], w_out.at[c], wout_sem.at[c]
        ).start()

    normed = (normalize(tokens[...].astype(F32)) * gain[...]).astype(BF16)
    for p in range(n_dp):
        nsend[p] = normed[:, p * depth : (p + 1) * depth]
    nrecv[me] = nsend[i]
    pl.semaphore_wait(barrier, n_dev - 1)

    def scatter_normed(d, carry):
        target = same_core(lax.rem(lane + d, n_lane))
        pltpu.make_async_remote_copy(
            src_ref=nsend.at[target[0]], dst_ref=nrecv.at[me],
            send_sem=a_send, recv_sem=a_recv.at[d],
            device_id=target, device_id_type=MESH,
        ).start()
        return carry

    def pass_on(source):
        pltpu.make_async_remote_copy(
            src_ref=nrecv.at[source], dst_ref=nrecv.at[source], send_sem=f_send, recv_sem=f_recv,
            device_id=sibling, device_id_type=MESH,
        ).start()

    lax.fori_loop(1, n_lane, scatter_normed, 0)
    pass_on(me)

    def forward_normed(d, carry):
        wait_bytes(nrecv.at[0], a_recv.at[d])
        source = same_core(lax.rem(lane + n_lane - d, n_lane))
        pass_on(source[0] * n_mp + source[1])
        return carry

    lax.fori_loop(1, n_lane, forward_normed, 0)
    wait_bytes(nrecv.at[pl.ds(0, n_lane)], f_recv)
    for s in range(n_dev):
        stage[s * rows : (s + 1) * rows, :] = nrecv[s].astype(F32)
    x[...] = stage[...].astype(BF16)

    def project(c, carry):
        pltpu.make_async_copy(w_query, w_in.at[c], win_sem.at[c]).wait()
        part = jnp.dot(x[...], w_in[c], preferred_element_type=F32).astype(BF16)
        psend[c] = part.reshape(n_dp, per, wide)
        precv[c, i] = psend[c, i]
        for d in range(1, n_dp):
            p = lax.rem(i + d, n_dp)
            pltpu.make_async_remote_copy(
                src_ref=psend.at[c, p], dst_ref=precv.at[c, i],
                send_sem=p_send, recv_sem=p_recv.at[c],
                device_id=(p, j), device_id_type=MESH,
            ).start()
        return carry

    lax.fori_loop(0, n_in, project, 0)

    def reduced(c):
        wait_bytes(precv.at[c, pl.ds(0, n_dp - 1)], p_recv.at[c])
        total = precv[c, 0].astype(F32)
        for p in range(1, n_dp):
            total = total + precv[c, p].astype(F32)
        return total

    def share(h, value):
        ag[h, i] = value
        for d in range(1, n_dp):
            p = lax.rem(i + d, n_dp)
            pltpu.make_async_remote_copy(
                src_ref=ag.at[h, i], dst_ref=ag.at[h, i],
                send_sem=g_send, recv_sem=g_recv.at[h],
                device_id=(p, j), device_id_type=MESH,
            ).start()

    query, key, value = reduced(0), reduced(1), reduced(2)
    mixed = []
    for h in range(wide // HEAD):
        cols = slice(h * HEAD, (h + 1) * HEAD)
        query_norm = normalize(query[:, cols].astype(BF16).astype(F32)).astype(BF16)
        key_norm = normalize(key[:, cols].astype(BF16).astype(F32)).astype(BF16)
        scores = lax.dot_general(
            query_norm, key_norm, (((1,), (1,)), ((), ())), preferred_element_type=F32
        )
        scores = scores * (temper[h] * (1.0 / math.sqrt(HEAD)))
        weight = jnp.exp(scores - jnp.max(scores, axis=-1, keepdims=True))
        probs = (weight / jnp.sum(weight, axis=-1, keepdims=True)).astype(BF16)
        mixed.append(
            jnp.dot(probs, value[:, cols].astype(BF16), preferred_element_type=F32).astype(BF16)
        )
    share(0, jnp.concatenate(mixed, axis=1))

    def activate(h, carry):
        at = pl.multiple_of((h - 1) * wide, HEAD)
        inner = reduced(h + 2) + bias[:, pl.ds(at, wide)]
        activ = 0.5 * inner * (1.0 + lax.erf(inner * math.sqrt(0.5)))
        share(h, activ.astype(BF16))
        return carry

    lax.fori_loop(1, n_out, activate, 0)

    acc[...] = jnp.zeros_like(acc)

    def project_out(h, carry):
        pltpu.make_async_copy(w_attn, w_out.at[h], wout_sem.at[h]).wait()
        wait_bytes(ag.at[h, pl.ds(0, n_dp - 1)], g_recv.at[h])
        acc[...] += jnp.dot(
            ag[h].reshape(n_dp * per, wide), w_out[h], preferred_element_type=F32
        ).reshape(acc.shape)
        return carry

    lax.fori_loop(0, n_out, project_out, 0)

    def halves(p, q):
        tile = acc[p, 2 * rows * q : 2 * rows * (q + 1), :]
        low, high = tile[:rows], tile[rows:]
        return jnp.where(core == 0, low, high), jnp.where(core == 0, high, low)

    for k in range(n_dp):
        p = lax.rem(i + 1 + k, n_dp)
        for q in range(n_chip):
            xsend[p, q] = halves(p, q)[1].astype(BF16)
        pltpu.make_async_remote_copy(
            src_ref=xsend.at[p], dst_ref=xrecv.at[p], send_sem=x_send, recv_sem=x_recv.at[k],
            device_id=sibling, device_id_type=MESH,
        ).start()

    for k in range(n_dp):
        p = lax.rem(i + 1 + k, n_dp)
        wait_bytes(xrecv.at[p], x_recv.at[k])
        for q in range(n_chip):
            dsend[p, q] = (halves(p, q)[0] + xrecv[p, q].astype(F32)).astype(BF16)

        def scatter_out(d, carry):
            q = lax.rem(chip + d, n_chip)
            pltpu.make_async_remote_copy(
                src_ref=dsend.at[p, q], dst_ref=drecv.at[lane], send_sem=d_send, recv_sem=d_recv,
                device_id=(p, 2 * q + core), device_id_type=MESH,
            ).start()
            return carry

        lax.fori_loop(1, n_chip if k == n_dp - 1 else n_chip + 1, scatter_out, 0)
    drecv[lane] = dsend[i, chip]
    wait_bytes(drecv.at[pl.ds(0, n_lane - 1)], d_recv)
    for p in range(n_dp):
        total = drecv[p * n_chip].astype(F32)
        for q in range(1, n_chip):
            total = total + drecv[p * n_chip + q].astype(F32)
        cols = slice(p * depth, (p + 1) * depth)
        out[:, cols] = (tokens[:, cols].astype(F32) + total).astype(BF16)

    wait_bytes(nrecv.at[pl.ds(0, n_lane - 1)], a_send)
    wait_bytes(nrecv.at[pl.ds(0, n_lane)], f_send)
    wait_bytes(precv.at[:, pl.ds(0, n_dp - 1)], p_send)
    wait_bytes(ag.at[:, pl.ds(0, n_dp - 1)], g_send)
    wait_bytes(xrecv, x_send)
    wait_bytes(drecv.at[pl.ds(0, n_lane - 1)], d_send)


def per_device(
    n_dp, n_mp,
    tokens, norm_gain, w_query, w_key, w_value, w_inner, bias_inner, w_attn_out, w_outer, temper
):
    rows, width = tokens.shape
    depth, wide = w_query.shape
    hidden = w_inner.shape[1]
    n_dev, per = n_dp * n_mp, n_mp * rows
    n_in, n_out = 3 + hidden // wide, 1 + hidden // wide
    vmem = pl.BlockSpec(memory_space=pltpu.VMEM)
    smem = pl.BlockSpec(memory_space=pltpu.SMEM)
    hbm = pl.BlockSpec(memory_space=pl.ANY)
    dma = pltpu.SemaphoreType.DMA
    return pl.pallas_call(
        functools.partial(block_kernel, n_dp, n_mp),
        out_shape=jax.ShapeDtypeStruct((rows, width), BF16),
        in_specs=[vmem, vmem, vmem, smem] + [hbm] * 6,
        out_specs=vmem,
        scratch_shapes=[
            pltpu.VMEM((n_in, depth, wide), BF16),
            pltpu.VMEM((n_out, wide, depth), BF16),
            pltpu.VMEM((n_dp, rows, depth), BF16),
            pltpu.VMEM((n_dev, rows, depth), BF16),
            pltpu.VMEM((n_dev * rows, depth), F32),
            pltpu.VMEM((n_dev * rows, depth), BF16),
            pltpu.VMEM((n_in, n_dp, per, wide), BF16),
            pltpu.VMEM((n_in, n_dp, per, wide), BF16),
            pltpu.VMEM((n_out, n_dp, per, wide), BF16),
            pltpu.VMEM((n_dp, per, depth), F32),
            pltpu.VMEM((n_dp, n_mp // 2, rows, depth), BF16),
            pltpu.VMEM((n_dp, n_mp // 2, rows, depth), BF16),
            pltpu.VMEM((n_dp, n_mp // 2, rows, depth), BF16),
            pltpu.VMEM((n_dev // 2, rows, depth), BF16),
            dma((n_in,)), dma((n_out,)), dma, dma((n_dev // 2,)), dma, dma, dma, dma((n_in,)),
            dma, dma((n_out,)), dma, dma((n_dp,)), dma, dma,
        ],
        compiler_params=pltpu.CompilerParams(
            collective_id=0, has_side_effects=True, vmem_limit_bytes=60 * 1024 * 1024
        ),
        name="encoder_block",
    )(
        tokens, norm_gain.reshape(1, -1), bias_inner.reshape(1, -1), temper,
        w_query, w_key, w_value, w_inner, w_attn_out, w_outer,
    )


def solution(mesh):
    return jax.shard_map(
        functools.partial(per_device, mesh.shape["dp"], mesh.shape["mp"]),
        mesh=mesh,
        in_specs=(
            P(("dp", "mp"), None),
            P(),
            P("dp", "mp"),
            P("dp", "mp"),
            P("dp", "mp"),
            P("dp", "mp"),
            P("mp"),
            P("mp", "dp"),
            P("mp", "dp"),
            P("mp"),
        ),
        out_specs=P(("dp", "mp"), None),
        check_vma=False,
    )
```

profile of v0, /device:TPU:1, one launch (start us, length us, event | category | flops | bytes accessed | tf_op | source)
XLA Modules:
  0.0 117.1 jit_solution(17656334438863942609)
XLA Ops:
  0.7 1.3 %reshape.7.bias = f32[1,768]{1,0:T(1,128)} reshape(f32[768]{0:T(1024)} %param.16) | data formatting | bytes 6144 | tf_op jit(solution)/shard_map/reshape | solution.py:267
  1.9 113.7 %encoder_block.1 = bf16[4,6144]{1,0:T(4,128)(2,1)} custom-call(bf16[4,6144]{1,0:T(4,128)(2,1)} %tokens.1, f32[1,6144]{1,0:T(1,128)} %bitcast.1, f32[1,768]{1,0:T(1,128)} %reshape.7.bias, f32[1]{0:T(128)S(6)} %copy.12.temper, bf16[768,128]{1,0:T(8,128)(2,1)} %w_query.1, bf16[768,128]{1,0:T(8,128)(2,1)} %w_key.1, bf16[768,128]{1,0:T(8,128)(2,1)} %w_value.1, ...), custom_call_target="tpu_custom_call" | custom-call | tf_op jit(solution)/shard_map/encoder_block/pallas_call | solution.py:239
  115.6 1.4 %copy.13 = bf16[4,6144]{1,0:T(4,128)(2,1)} copy(bf16[4,6144]{1,0:T(4,128)(2,1)} %encoder_block.1) | data formatting | bytes 98304
where the time goes:
time: 117 us
  Pallas kernels  114 us (97%)
  local copies, waits for them, and re-layouts  2.7 us (2%)
    pallas_call x1, Pallas kernels, per_device(): pl.pallas_call(functools.partial(block_kernel, n_dp, n_mp), out_shape=jax...  114 us

commit v1 on v0

v1 whole, which is shorter than its diff:
```python
import functools
import math

import jax
import jax.numpy as jnp
from jax import lax
from jax.experimental import pallas as pl
from jax.experimental.pallas import tpu as pltpu
from jax.sharding import PartitionSpec as P

HEAD = 128
NX, NY, NZ = 2, 4, 8
MESH = pl.DeviceIdType.MESH
F32, BF16 = jnp.float32, jnp.bfloat16


def normalize(values):
    center = values - jnp.mean(values, axis=-1, keepdims=True)
    spread = jnp.mean(center * center, axis=-1, keepdims=True)
    return center * lax.rsqrt(spread + 1e-06)


def wait_bytes(ref, sem):
    pltpu.make_async_copy(ref, ref, sem).wait()


def block_kernel(
    tokens, gain, bias, temper, w_query, w_key, w_value, w_inner, w_attn, w_outer,
    out,
    w_qkv, w_in, w_at, w_out, nsend, nrecv, stage, xg, pf, asend, arecv, brsend, brrecv,
    blsend, blrecv, sf, csend, crecv, qkv, ag, mg, og, esend, erecv, rsend, rrecv, fsend, frecv,
    win_sem, n_send, n_recv, m_send, m_recv, r_send, r_recv, s_send, s_recv,
    a_send, ar_recv, al_recv, b_send, br_recv, bl_recv, c_send, c_recv,
    gx_send, gx_recv, gy_send, gr_recv, gl_recv, h_send, hr_recv, hl_recv,
    e_send, e_recv, z_send, z_recv, f_send, f_recv,
):
    rows, depth = nsend.shape[1:]
    wide = w_qkv.shape[1]
    full = pf.shape[3]
    cut = 5 * HEAD
    half = depth // 2
    i, j = lax.axis_index("dp"), lax.axis_index("mp")
    xl, y = i // NY, lax.rem(i, NY)
    z, xh, c = j // 4, lax.rem(j // 2, 2), lax.rem(j, 2)
    yr, yl, y2 = lax.rem(y + 1, NY), lax.rem(y + NY - 1, NY), lax.rem(y + 2, NY)
    zr, zl = lax.rem(z + 1, NZ), lax.rem(z + NZ - 1, NZ)
    sibling = (i, z * 4 + xh * 2 + 1 - c)
    partner = ((1 - xl) * NY + y, j)
    y_right, y_left = (xl * NY + yr, j), (xl * NY + yl, j)
    z_right, z_left = (i, zr * 4 + xh * 2 + c), (i, zl * 4 + xh * 2 + c)

    def send(src, dst, send_sem, recv_sem, target):
        pltpu.make_async_remote_copy(
            src_ref=src, dst_ref=dst, send_sem=send_sem, recv_sem=recv_sem,
            device_id=target, device_id_type=MESH,
        ).start()

    barrier = pltpu.get_barrier_semaphore()
    n_plane = 4 * NX * NY
    here = i * 4 + xh * 2 + c

    def greet(d, carry):
        t = lax.rem(here + d, n_plane)
        pl.semaphore_signal(
            barrier, inc=1, device_id=(t // 4, z * 4 + lax.rem(t, 4)), device_id_type=MESH
        )
        return carry

    lax.fori_loop(1, n_plane, greet, 0)
    for target in (z_right, z_left):
        pl.semaphore_signal(barrier, inc=1, device_id=target, device_id_type=MESH)

    loads = [
        pltpu.make_async_copy(w, w_qkv.at[:, n * HEAD : (n + 1) * HEAD], win_sem.at[n])
        for n, w in enumerate((w_query, w_key, w_value))
    ]
    loads.append(pltpu.make_async_copy(w_inner, w_in, win_sem.at[3]))
    loads.append(pltpu.make_async_copy(w_attn, w_at, win_sem.at[4]))
    loads.append(pltpu.make_async_copy(w_outer, w_out, win_sem.at[5]))
    for load in loads:
        load.start()

    normed = (normalize(tokens[...].astype(F32)) * gain[...]).astype(BF16)
    for p in range(NX * NY):
        nsend[p] = normed[:, p * depth : (p + 1) * depth]
    lane = i * 2 + xh
    nrecv[c, lane] = nsend[i]
    pl.semaphore_wait(barrier, n_plane + 1)

    n_lane = 2 * NX * NY

    def scatter_normed(d, carry):
        t = lax.rem(lane + d, n_lane)
        send(
            nsend.at[t // 2], nrecv.at[c, lane], n_send, n_recv,
            (t // 2, z * 4 + lax.rem(t, 2) * 2 + c),
        )
        return carry

    lax.fori_loop(1, n_lane, scatter_normed, 0)
    wait_bytes(nrecv.at[0, pl.ds(0, n_lane - 1)], n_recv)
    send(nrecv.at[c], nrecv.at[c], m_send, m_recv, sibling)
    wait_bytes(nrecv.at[0], m_recv)
    for q in range(NX * NY):
        p = q % NX * NY + q // NX
        for s in range(4):
            at = q * 4 * rows + s * rows
            stage[at : at + rows, :] = nrecv[s % 2, p * 2 + s // 2].astype(F32)
    xg[0] = stage[...].astype(BF16).reshape(xg.shape[1:])

    def ring_right(src, dst):
        send(xg.at[src, c], xg.at[dst, c], r_send, r_recv.at[dst], z_right)

    def ring_left(src, dst):
        send(xg.at[src, c], xg.at[dst, c], r_send, r_recv.at[dst], z_left)

    def ring(d):
        top, low = pl.ds(0, 8 * rows), pl.ds(8 * rows, 8 * rows)
        if d == 0:
            ring_right(0, 7)
            ring_left(0, 1)
            return
        if d == 4:
            wait_bytes(xg.at[4, 0, top], r_recv.at[4])
            wait_bytes(xg.at[4, 0, low], r_recv.at[8])
            send(xg.at[4, c], xg.at[4, c], s_send, s_recv.at[4], sibling)
            return
        wait_bytes(xg.at[8 - d, 0], r_recv.at[8 - d])
        if d < 3:
            ring_right(8 - d, 7 - d)
        else:
            send(xg.at[5, c, top], xg.at[4, c, top], r_send, r_recv.at[4], z_right)
        send(xg.at[8 - d, c], xg.at[8 - d, c], s_send, s_recv.at[8 - d], sibling)
        wait_bytes(xg.at[d, 0], r_recv.at[d])
        if d < 3:
            ring_left(d, d + 1)
        else:
            send(xg.at[3, c, low], xg.at[4, c, low], r_send, r_recv.at[8], z_left)
        send(xg.at[d, c], xg.at[d, c], s_send, s_recv.at[d], sibling)

    units = [(0,), (7, 1), (6, 2), (5, 3), (4,)]

    def project(k):
        if k != 0:
            wait_bytes(xg.at[k, 0], s_recv.at[k])
        x = xg[k].reshape(32 * rows, depth)
        pf[k, :, :, :wide] = jnp.dot(
            x, w_qkv[...], preferred_element_type=F32
        ).reshape(NY, 8 * rows, wide)
        pf[k, :, :, wide:] = jnp.dot(
            x, w_in[...], preferred_element_type=F32
        ).reshape(NY, 8 * rows, full - wide)

    def stage_a(k):
        asend[k] = pf[k, y2].astype(BF16)
        right, left = pl.ds(0, cut), pl.ds(cut, full - cut)
        send(asend.at[k, :, right], arecv.at[k, :, right], a_send, ar_recv.at[k], y_right)
        send(asend.at[k, :, left], arecv.at[k, :, left], a_send, al_recv.at[k], y_left)

    def stage_b(k):
        wait_bytes(arecv.at[k, :, pl.ds(0, cut)], ar_recv.at[k])
        brsend[k, :, :cut] = (pf[k, yr, :, :cut] + arecv[k, :, :cut].astype(F32)).astype(BF16)
        brsend[k, :, cut:] = pf[k, yr, :, cut:].astype(BF16)
        send(brsend.at[k], brrecv.at[k], b_send, br_recv.at[k], y_right)
        wait_bytes(arecv.at[k, :, pl.ds(cut, full - cut)], al_recv.at[k])
        blsend[k, :, :cut] = pf[k, yl, :, :cut].astype(BF16)
        blsend[k, :, cut:] = (pf[k, yl, :, cut:] + arecv[k, :, cut:].astype(F32)).astype(BF16)
        send(blsend.at[k], blrecv.at[k], b_send, bl_recv.at[k], y_left)

    def stage_c(k):
        wait_bytes(brrecv.at[k], br_recv.at[k])
        wait_bytes(blrecv.at[k], bl_recv.at[k])
        total = pf[k, y] + brrecv[k].astype(F32) + blrecv[k].astype(F32)
        low, high = total[: 4 * rows], total[4 * rows :]
        csend[k] = jnp.where(xl == 0, high, low).astype(BF16)
        send(csend.at[k], crecv.at[k], c_send, c_recv.at[k], partner)
        sf[k] = jnp.where(xl == 0, low, high)

    def stage_d(k):
        wait_bytes(crecv.at[k], c_recv.at[k])
        total = sf[k] + crecv[k].astype(F32)
        qkv[k] = total[:, :wide].astype(BF16)
        inner = total[:, wide:] + bias[...]
        activ = 0.5 * inner * (1.0 + lax.erf(inner * math.sqrt(0.5)))
        ag[k, y, xl] = activ.astype(BF16)
        send(ag.at[k, y, xl], ag.at[k, y, xl], gx_send, gx_recv.at[k], partner)

    def gather_y(g, k, at):
        wait_bytes(g.at[at + (0, 0)], gx_recv.at[k])
        send(g.at[at + (y,)], g.at[at + (y,)], gy_send, gr_recv.at[k], y_right)
        send(g.at[at + (y,)], g.at[at + (y,)], gy_send, gl_recv.at[k], y_left)

    def gather_far(g, k, at):
        wait_bytes(g.at[at + (0,)], gr_recv.at[k])
        send(g.at[at + (yl, 0)], g.at[at + (yl, 0)], h_send, hr_recv.at[k], y_right)
        wait_bytes(g.at[at + (0,)], gl_recv.at[k])
        send(g.at[at + (yr, 1)], g.at[at + (yr, 1)], h_send, hl_recv.at[k], y_left)

    def gather_done(g, k, at):
        wait_bytes(g.at[at + (0, 0)], hr_recv.at[k])
        wait_bytes(g.at[at + (0, 0)], hl_recv.at[k])

    def each(stage_fn, u):
        if 0 <= u < len(units):
            for k in units[u]:
                stage_fn(k)

    def attend():
        query = qkv[:, :, :HEAD].reshape(32 * rows, HEAD)
        key = qkv[:, :, HEAD : 2 * HEAD].reshape(32 * rows, HEAD)
        value = qkv[:, :, 2 * HEAD :].reshape(32 * rows, HEAD)
        query_norm = normalize(query.astype(F32)).astype(BF16)
        key_norm = normalize(key.astype(F32)).astype(BF16)
        scores = lax.dot_general(
            query_norm, key_norm, (((1,), (1,)), ((), ())), preferred_element_type=F32
        )
        scores = scores * (temper[0] * (1.0 / math.sqrt(HEAD)))
        weight = jnp.exp(scores - jnp.max(scores, axis=-1, keepdims=True))
        probs = (weight / jnp.sum(weight, axis=-1, keepdims=True)).astype(BF16)
        mg[y, xl] = jnp.dot(probs, value, preferred_element_type=F32).astype(BF16)
        send(mg.at[y, xl], mg.at[y, xl], gx_send, gx_recv.at[8], partner)

    ring(0)
    for load in loads[:4]:
        load.wait()
    for u in range(len(units) + 6):
        if 1 <= u <= 4:
            ring(u)
        each(stage_b, u - 1)
        each(stage_c, u - 2)
        each(stage_d, u - 3)
        if u - 3 == 4:
            attend()
        each(lambda k: gather_y(ag, k, (k,)), u - 4)
        if u - 4 == 4:
            gather_y(mg, 8, ())
        each(lambda k: gather_far(ag, k, (k,)), u - 5)
        if u - 5 == 4:
            gather_far(mg, 8, ())
        if u < 5:
            each(project, u)
            each(stage_a, u)

    for load in loads[4:]:
        load.wait()
    gather_done(mg, 8, ())

    def project_out(k):
        gather_done(ag, k, (k,))
        hidden = ag[k].reshape(32 * rows, depth)
        mixed = mg[:, :, 4 * rows * k : 4 * rows * (k + 1), :].reshape(32 * rows, HEAD)
        total = jnp.dot(hidden, w_out[...], preferred_element_type=F32)
        total = total + jnp.dot(mixed, w_at[...], preferred_element_type=F32)
        og[k] = total.reshape(og.shape[1:])
        esend[k] = og[k, 1 - c].astype(BF16)
        send(esend.at[k], erecv.at[k], e_send, e_recv.at[k], sibling)

    def combined(k):
        wait_bytes(erecv.at[k], e_recv.at[k])
        return og[k, c] + erecv[k].astype(F32)

    low, high = pl.ds(0, half), pl.ds(half, half)

    def reduce_out(k):
        total = combined(k)
        if k == 4:
            rsend[4] = total.astype(BF16)
            send(rsend.at[4, :, low], rrecv.at[3, :, low], z_send, z_recv.at[3], z_right)
            send(rsend.at[4, :, high], rrecv.at[5, :, high], z_send, z_recv.at[5], z_left)
            return
        if k == 3:
            wait_bytes(rrecv.at[3, :, low], z_recv.at[3])
            rsend[3, :, :half] = (total[:, :half] + rrecv[3, :, :half].astype(F32)).astype(BF16)
            rsend[3, :, half:] = total[:, half:].astype(BF16)
        elif k == 5:
            wait_bytes(rrecv.at[5, :, high], z_recv.at[5])
            rsend[5, :, :half] = total[:, :half].astype(BF16)
            rsend[5, :, half:] = (total[:, half:] + rrecv[5, :, half:].astype(F32)).astype(BF16)
        else:
            wait_bytes(rrecv.at[k], z_recv.at[k])
            rsend[k] = (total + rrecv[k].astype(F32)).astype(BF16)
        to = k - 1 if k < 4 else k + 1
        send(rsend.at[k], rrecv.at[to], z_send, z_recv.at[to], z_right if k < 4 else z_left)

    order = [(4,), (5, 3), (6, 2), (7, 1), (0,)]
    for u in range(6):
        if u < 5:
            for k in order[u]:
                project_out(k)
        if u >= 1 and u < 5:
            for k in order[u - 1]:
                reduce_out(k)
    total = combined(0)
    wait_bytes(rrecv.at[0], z_recv.at[0])
    wait_bytes(rrecv.at[8], z_recv.at[8])
    total = total + rrecv[0].astype(F32) + rrecv[8].astype(F32)
    mine = c == y // 2
    for q in range(4):
        for s in range(4):
            at = q * 4 * rows + s * rows
            fsend[q * 4 + s] = total[at : at + rows].astype(BF16)
    for q in range(4):
        p = q % NX * NY + 2 * c + q // NX
        for s in range(4):
            own = jnp.logical_and(p == i, s == xh * 2 + c)

            @pl.when(own)
            def _():
                frecv[i * 2 + xh] = fsend[q * 4 + s]

            @pl.when(jnp.logical_not(own))
            def _():
                send(fsend.at[q * 4 + s], frecv.at[i * 2 + xh], f_send, f_recv, (p, z * 4 + s))

    @pl.when(mine)
    def _():
        wait_bytes(frecv.at[pl.ds(0, n_lane - 1)], f_recv)
        wait_bytes(frecv.at[pl.ds(0, n_lane - 1)], f_send)

    @pl.when(jnp.logical_not(mine))
    def _():
        wait_bytes(frecv, f_recv)
        wait_bytes(frecv, f_send)

    for p in range(NX * NY):
        cols = slice(p * depth, (p + 1) * depth)
        total = frecv[2 * p].astype(F32) + frecv[2 * p + 1].astype(F32)
        out[:, cols] = (tokens[:, cols].astype(F32) + total).astype(BF16)

    wait_bytes(nrecv.at[0, pl.ds(0, n_lane - 1)], n_send)
    wait_bytes(nrecv.at[0], m_send)
    wait_bytes(xg.at[pl.ds(0, 7), 0], r_send)
    wait_bytes(xg.at[pl.ds(0, 7), 0], s_send)
    wait_bytes(asend, a_send)
    wait_bytes(brsend, b_send)
    wait_bytes(blsend, b_send)
    wait_bytes(csend, c_send)
    wait_bytes(ag.at[:, 0, 0], gx_send)
    wait_bytes(mg.at[0, 0], gx_send)
    wait_bytes(ag.at[:, pl.ds(0, 2)], gy_send)
    wait_bytes(mg.at[pl.ds(0, 2)], gy_send)
    wait_bytes(ag.at[:, 0], h_send)
    wait_bytes(mg.at[0], h_send)
    wait_bytes(esend, e_send)
    wait_bytes(rsend.at[pl.ds(0, 7)], z_send)


def per_device(
    tokens, norm_gain, w_query, w_key, w_value, w_inner, bias_inner, w_attn_out, w_outer, temper
):
    rows, width = tokens.shape
    depth = w_query.shape[0]
    wide = 3 * HEAD
    hidden = w_inner.shape[1]
    full = wide + hidden
    vmem = pl.BlockSpec(memory_space=pltpu.VMEM)
    smem = pl.BlockSpec(memory_space=pltpu.SMEM)
    hbm = pl.BlockSpec(memory_space=pl.ANY)
    dma = pltpu.SemaphoreType.DMA
    block = 8 * rows
    return pl.pallas_call(
        block_kernel,
        out_shape=jax.ShapeDtypeStruct((rows, width), BF16),
        in_specs=[vmem, vmem, vmem, smem] + [hbm] * 6,
        out_specs=vmem,
        scratch_shapes=[
            pltpu.VMEM((depth, wide), BF16),
            pltpu.VMEM((depth, hidden), BF16),
            pltpu.VMEM((HEAD, depth), BF16),
            pltpu.VMEM((hidden, depth), BF16),
            pltpu.VMEM((8, rows, depth), BF16),
            pltpu.VMEM((2, 16, rows, depth), BF16),
            pltpu.VMEM((32 * rows, depth), F32),
            pltpu.VMEM((NZ, 2, 16 * rows, depth), BF16),
            pltpu.VMEM((NZ, NY, block, full), F32),
            pltpu.VMEM((NZ, block, full), BF16),
            pltpu.VMEM((NZ, block, full), BF16),
            pltpu.VMEM((NZ, block, full), BF16),
            pltpu.VMEM((NZ, block, full), BF16),
            pltpu.VMEM((NZ, block, full), BF16),
            pltpu.VMEM((NZ, block, full), BF16),
            pltpu.VMEM((NZ, 4 * rows, full), F32),
            pltpu.VMEM((NZ, 4 * rows, full), BF16),
            pltpu.VMEM((NZ, 4 * rows, full), BF16),
            pltpu.VMEM((NZ, 4 * rows, wide), BF16),
            pltpu.VMEM((NZ, NY, NX, 4 * rows, hidden), BF16),
            pltpu.VMEM((NY, NX, 32 * rows, HEAD), BF16),
            pltpu.VMEM((NZ, 2, 16 * rows, depth), F32),
            pltpu.VMEM((NZ, 16 * rows, depth), BF16),
            pltpu.VMEM((NZ, 16 * rows, depth), BF16),
            pltpu.VMEM((NZ, 16 * rows, depth), BF16),
            pltpu.VMEM((NZ + 1, 16 * rows, depth), BF16),
            pltpu.VMEM((16, rows, depth), BF16),
            pltpu.VMEM((16, rows, depth), BF16),
            dma((6,)), dma, dma, dma, dma, dma, dma((9,)), dma, dma((8,)),
            dma, dma((8,)), dma((8,)), dma, dma((8,)), dma((8,)), dma, dma((8,)),
            dma, dma((9,)), dma, dma((9,)), dma((9,)), dma, dma((9,)), dma((9,)),
            dma, dma((8,)), dma, dma((9,)), dma, dma,
        ],
        compiler_params=pltpu.CompilerParams(
            collective_id=0, has_side_effects=True, vmem_limit_bytes=60 * 1024 * 1024
        ),
        name="encoder_block",
    )(
        tokens, norm_gain.reshape(1, -1), bias_inner.reshape(1, -1), temper,
        w_query, w_key, w_value, w_inner, w_attn_out, w_outer,
    )


def solution(mesh):
    return jax.shard_map(
        per_device,
        mesh=mesh,
        in_specs=(
            P(("dp", "mp"), None),
            P(),
            P("dp", "mp"),
            P("dp", "mp"),
            P("dp", "mp"),
            P("dp", "mp"),
            P("mp"),
            P("mp", "dp"),
            P("mp", "dp"),
            P("mp"),
        ),
        out_specs=P(("dp", "mp"), None),
        check_vma=False,
    )
```

time: 117 us -> 93 us (0.79)
  Pallas kernels: 114 us -> 89.4 us
    pallas_call x1, Pallas kernels: 114 us -> 89.4 us  [per_device(): pl.pallas_call(block_kernel, out_shape=jax.ShapeDtypeStruct((rows, width)...]
where the time goes in v1:
time: 93 us; the launch traced here: 92.8 us
  Pallas kernels  89.4 us (96%)
  local copies, waits for them, and re-layouts  2.7 us (3%)
    pallas_call x1, Pallas kernels, per_device(): pl.pallas_call(block_kernel, out_shape=jax.ShapeDtypeStruct((rows, width)...  89.4 us

profile of v1, /device:TPU:1, one launch (start us, length us, event | category | flops | bytes accessed | tf_op | source)
XLA Modules:
  0.0 92.8 jit_solution(9684696367956293291)
XLA Ops:
  0.7 1.3 %reshape.7.bias = f32[1,768]{1,0:T(1,128)} reshape(f32[768]{0:T(1024)} %param.16) | data formatting | bytes 6144 | tf_op jit(solution)/shard_map/reshape | solution.py:405
  1.9 89.4 %encoder_block.1 = bf16[4,6144]{1,0:T(4,128)(2,1)} custom-call(bf16[4,6144]{1,0:T(4,128)(2,1)} %tokens.1, f32[1,6144]{1,0:T(1,128)} %bitcast.1, f32[1,768]{1,0:T(1,128)} %reshape.7.bias, f32[1]{0:T(128)S(6)} %copy.12.temper, bf16[768,128]{1,0:T(8,128)(2,1)} %w_query.1, bf16[768,128]{1,0:T(8,128)(2,1)} %w_key.1, bf16[768,128]{1,0:T(8,128)(2,1)} %w_value.1, ...), custom_call_target="tpu_custom_call" | custom-call | tf_op jit(solution)/shard_map/encoder_block/pallas_call | solution.py:361
  91.3 1.4 %copy.13 = bf16[4,6144]{1,0:T(4,128)(2,1)} copy(bf16[4,6144]{1,0:T(4,128)(2,1)} %encoder_block.1) | data formatting | bytes 98304

commit v2 on v0

v2 whole, which is shorter than its diff:
```python
import functools
import math

import jax
import jax.numpy as jnp
from jax import lax
from jax.experimental import pallas as pl
from jax.experimental.pallas import tpu as pltpu
from jax.sharding import PartitionSpec as P

HEAD = 128
NX, NY, NZ = 2, 4, 8
MESH = pl.DeviceIdType.MESH
F32, BF16 = jnp.float32, jnp.bfloat16
GROUPS = ((0, 384, "x"), (384, 1152, "y"))
REDUCE_AT_ONCE = ((), (5,))
REDUCE_IN_TWO = (0, 4)
GATHER_AT_ONCE = (4, 7, 8)
GATHER_IN_TWO = (1,)
Y_FIRST = (5, 6)
PEERS = tuple((dx, dy) for dy in (2, 1, 3, 0) for dx in (1, 0) if dx or dy)
SCHEDULE = (
    "r.0", "w0.0", "p0.0", "p1.0", "b.1", "r0.1", "p0.1", "r1.1", "q0.0", "b.7",
    "r0.7", "p0.7", "m0.0", "q0.7", "r1.7", "p1.1", "r0.2", "q0.1", "m0.1", "r0.6",
    "q1.0", "p1.7", "r1.2", "m0.7", "q1.7", "r1.6", "p0.2", "p1.2", "q0.2", "m0.2",
    "m1.0", "p0.6", "m1.1", "p1.6", "m0.6", "q0.6", "r0.3", "r0.5", "q1.1", "q2.7",
    "q2.0", "r1.3", "r1.5", "m1.2", "p0.3", "q0.3", "p0.5", "q0.5", "p1.5", "q1.2",
    "m0.5", "q1.6", "r.4", "q3.0", "p1.3", "m0.3", "p0.4", "p1.4", "m0.4", "q0.4",
    "q1.5", "m2.0", "m2.1", "q1.3", "m1.6", "m1.3", "q1.4", "m2.2", "q2.2", "q2.6",
    "q3.7", "y.0", "m1.4", "m1.5", "q2.1", "q2.5", "q2.3", "m3.1", "q2.4", "m1.7",
    "m2.3", "q3.2", "m2.6", "m2.4", "q3.3", "q3.6", "y.5", "q3.4", "m3.3", "q3.1",
    "q3.5", "m3.2", "m3.6", "a.0", "y.3", "y.6", "m2.7", "f.5", "g0.0", "y.2",
    "f.3", "g1.0", "w1.0", "o.4", "f.6", "f.0", "s1.4", "s0.4", "f.2", "o.5",
    "m3.7", "y.1", "o.3", "s0.5", "o.0", "s1.3", "s1.5", "s0.3", "o.6", "o.2",
    "s0.6", "s1.2", "s1.6", "s0.2", "o.7", "o.1", "s0.7", "s0.1",
)
OFFSETS = sorted(
    ((dx, dy) for dx in range(4) for dy in range(NY)),
    key=lambda o: -(min(o[0], 4 - o[0]) + min(o[1], NY - o[1])),
)

scope = jax.named_scope


def normalize(values):
    center = values - jnp.mean(values, axis=-1, keepdims=True)
    spread = jnp.mean(center * center, axis=-1, keepdims=True)
    return center * lax.rsqrt(spread + 1e-06)


def wait_bytes(ref, sem):
    pltpu.make_async_copy(ref, ref, sem).wait()


def send(src, dst, send_sem, recv_sem, target):
    pltpu.make_async_remote_copy(
        src_ref=src, dst_ref=dst, send_sem=send_sem, recv_sem=recv_sem,
        device_id=target, device_id_type=MESH,
    ).start()


def block_kernel(
    tokens_ref, gain_ref, bias_ref, temper, w_query, w_key, w_value, w_inner, w_attn, w_outer,
    out,
    tokens, gain, bias, w_qkv, w_in, w_at, w_out, nsend, nrecv, stage, xg, pf, groups,
    direct, qkv, ag, mg, og, esend, erecv, rsend, rrecv, fsend, frecv,
    in_sem, win_sem, n_send, n_recv, m_send, m_recv, r_send, r_recv, s_send, s_recv,
    gd_send, gd_recv, gx_send, gx_recv, gy_send, gr_recv, gl_recv, h_send, hr_recv, hl_recv,
    e_send, e_recv, z_send, z_recv, f_send, f_recv,
):
    rows, depth = nsend.shape[1:]
    tile = 4 * rows
    half = depth // 2
    i, j = lax.axis_index("dp"), lax.axis_index("mp")
    xl, y = i // NY, lax.rem(i, NY)
    z, xh, c = j // 4, lax.rem(j // 2, 2), lax.rem(j, 2)
    x, me = xh * 2 + xl, y * NX + xl
    yr, yl, y2 = lax.rem(y + 1, NY), lax.rem(y + NY - 1, NY), lax.rem(y + 2, NY)
    zr, zl = lax.rem(z + 1, NZ), lax.rem(z + NZ - 1, NZ)
    sibling = (i, z * 4 + xh * 2 + 1 - c)
    partner = ((1 - xl) * NY + y, j)
    y_right, y_left = (xl * NY + yr, j), (xl * NY + yl, j)
    z_right, z_left = (i, zr * 4 + xh * 2 + c), (i, zl * 4 + xh * 2 + c)

    planes = (z, zl, zr)

    def in_plane(dx, to_y, core, n=0):
        to = lax.rem(x + dx, 4)
        return (lax.rem(to, 2) * NY + to_y, planes[n] * 4 + (to // 2) * 2 + core)

    inputs = [
        pltpu.make_async_copy(src, dst, in_sem.at[n])
        for n, (src, dst) in enumerate(((tokens_ref, tokens), (gain_ref, gain), (bias_ref, bias)))
    ]
    for load in inputs:
        load.start()
    barrier = pltpu.get_barrier_semaphore()

    with scope("greet"):
        for dx, dy in OFFSETS:
            to_y = lax.rem(y + dy, NY)
            for core, n in ((c, 1), (c, 2), (c, 0), (1 - c, 1), (1 - c, 2), (1 - c, 0)):
                if n == 0 and dx == 0 and dy == 0 and core is c:
                    continue
                pl.semaphore_signal(
                    barrier, inc=1, device_id=in_plane(dx, to_y, core, n), device_id_type=MESH
                )

    loads = [
        pltpu.make_async_copy(w, w_qkv.at[:, n * HEAD : (n + 1) * HEAD], win_sem.at[n])
        for n, w in enumerate((w_query, w_key, w_value))
    ]
    loads.append(pltpu.make_async_copy(w_inner, w_in, win_sem.at[3]))
    loads.append(pltpu.make_async_copy(w_attn, w_at, win_sem.at[4]))
    loads.append(pltpu.make_async_copy(w_outer, w_out, win_sem.at[5]))
    for load in loads:
        load.start()
    for load in inputs:
        load.wait()

    with scope("norm"):
        normed = (normalize(tokens[...].astype(F32)) * gain[...]).astype(BF16)
        for p in range(NX * NY):
            nsend[p] = normed[:, p * depth : (p + 1) * depth]
        lane = i * 2 + xh
        nrecv[0, c, lane] = nsend[i]
    with scope("barrier"):
        pl.semaphore_wait(barrier, 12 * NX * NY - 1)

    n_lane = 2 * NX * NY
    with scope("plane"):
        for n in (0, 1, 2):
            for dx, dy in OFFSETS:
                if n == 0 and dx == 0 and dy == 0:
                    continue
                target = in_plane(dx, lax.rem(y + dy, NY), c, n)
                send(nsend.at[target[0]], nrecv.at[n, c, lane], n_send, n_recv.at[n], target)

    def share_plane(n):
        wait_bytes(nrecv.at[n, 0, pl.ds(0, n_lane - (n == 0))], n_recv.at[n])
        send(nrecv.at[n, c], nrecv.at[n, c], m_send, m_recv.at[n], sibling)

    def build(n, k):
        wait_bytes(nrecv.at[n, 0], m_recv.at[n])
        for q in range(NX * NY):
            p = q % NX * NY + q // NX
            for s in range(4):
                at = q * tile + s * rows
                stage[n, at : at + rows, :] = nrecv[n, s % 2, p * 2 + s // 2].astype(F32)
        xg[k] = stage[n].astype(BF16).reshape(xg.shape[1:])

    cols = (pl.ds(0, half), pl.ds(half, half))
    piece = 8 * rows
    parts = (pl.ds(0, piece), pl.ds(piece, piece))

    def pass_on(src, dst, n, target):
        send(
            xg.at[src, c, parts[n]], xg.at[dst, c, parts[n]], r_send, r_recv.at[dst, n], target
        )

    def ring(k, n):
        if k == 0:
            for n in (0, 1, 2):
                share_plane(n)
                if n == 0:
                    build(0, 0)
            return
        if k == 4:
            for n in (0, 1):
                wait_bytes(xg.at[4, 0, parts[n]], r_recv.at[4, n])
            send(xg.at[4, c], xg.at[4, c], s_send, s_recv.at[4], sibling)
            return
        if k not in (1, 7):
            wait_bytes(xg.at[k, 0, parts[n]], r_recv.at[k, n])
        if k not in (3, 5) or (k, n) in ((5, 0), (3, 1)):
            pass_on(k, k - 1 if k > 4 else k + 1, n, z_right if k > 4 else z_left)
        if n == 1 and k not in (1, 7):
            send(xg.at[k, c], xg.at[k, c], s_send, s_recv.at[k], sibling)

    def project(g, k):
        low, high, _ = GROUPS[g]
        if k not in (0, 1, 7) and g == 0:
            wait_bytes(xg.at[k, 0], s_recv.at[k])
        w = w_qkv[...] if g == 0 else w_in[:, low - 384 : high - 384]
        pf[k, :, :, :, low:high] = jnp.dot(
            xg[k].reshape(8 * tile, depth), w, preferred_element_type=F32
        ).reshape(NY, NX, tile, high - low)

    def finish(g, k, total):
        low, high, _ = GROUPS[g]
        if g == 0:
            qkv[k] = total.astype(BF16)
            return
        low, high = low - 384, high - 384
        shift = jnp.concatenate([bias[h : h + 1] for h in range(low // HEAD, high // HEAD)], axis=1)
        inner = total + shift
        activ = 0.5 * inner * (1.0 + lax.erf(inner * math.sqrt(0.5)))
        ag[k, me, :, low:high] = activ.astype(BF16)
        if k in GATHER_AT_ONCE:
            gather_all(ag, (k,), k)
        elif k in Y_FIRST and k not in GATHER_IN_TWO:
            block = ag.at[k, me]
            send(block, block, gy_send, gr_recv.at[k], y_right)
            send(block, block, gy_send, gl_recv.at[k], y_left)
        else:
            send(ag.at[k, me], ag.at[k, me], gx_send, gx_recv.at[k], partner)

    def slices(g, k):
        width = GROUPS[g][1] - GROUPS[g][0]
        cut = (width // HEAD + k % 2) // 2 * HEAD
        return cut, pl.ds(0, cut), pl.ds(cut, width - cut)

    def start_ring(g, k, far):
        asend, arecv, _, _, _, _, a_send, ar, al, _, _, _ = groups[g][:12]
        _, right, left = slices(g, k)
        asend[k] = far.astype(BF16)
        at = (k,) + (slice(None),) * (len(asend.shape) - 2)
        send(asend.at[at + (right,)], arecv.at[at + (right,)], a_send, ar.at[k], y_right)
        send(asend.at[at + (left,)], arecv.at[at + (left,)], a_send, al.at[k], y_left)

    def relay(g, k, block):
        _, arecv, brs, brr, bls, blr, _, ar, al, b_send, br, bl = groups[g][:12]
        cut, right, left = slices(g, k)
        at = (k,) + (slice(None),) * (len(arecv.shape) - 2)
        value = block(yr)
        wait_bytes(arecv.at[at + (right,)], ar.at[k])
        brs[k] = jnp.concatenate(
            [value[..., :cut] + arecv[at + (slice(0, cut),)].astype(F32), value[..., cut:]], axis=-1
        ).astype(BF16)
        send(brs.at[k], brr.at[k], b_send, br.at[k], y_right)
        value = block(yl)
        wait_bytes(arecv.at[at + (left,)], al.at[k])
        bls[k] = jnp.concatenate(
            [value[..., :cut], value[..., cut:] + arecv[at + (slice(cut, None),)].astype(F32)], axis=-1
        ).astype(BF16)
        send(bls.at[k], blr.at[k], b_send, bl.at[k], y_left)

    def arrived(g, k, block):
        _, _, _, brr, _, blr, _, _, _, _, br, bl = groups[g][:12]
        wait_bytes(brr.at[k], br.at[k])
        wait_bytes(blr.at[k], bl.at[k])
        return block(y) + brr[k].astype(F32) + blr[k].astype(F32)

    def reduce_two(k, step):
        low, high, _ = GROUPS[1]
        dsend, drecv, d_send, d_recv = direct[1]
        sf, xsend, xrecv, x_send, x_recv = groups[1][12:]
        if step == 0:
            dsend[k] = pf[k, :, :, :, low:high].reshape(dsend.shape[1:]).astype(BF16)
            for n, to in enumerate((y2, yr, yl)):
                send(
                    dsend.at[k, pl.ds(to * NX, NX)], drecv.at[k, pl.ds(n * NX, NX)],
                    d_send, d_recv.at[k], (xl * NY + to, j),
                )
        elif step == 1:
            wait_bytes(drecv.at[k, pl.ds(0, 3 * NX)], d_recv.at[k])
            total = pf[k, y, :, :, low:high]
            for n in range(3):
                total = total + drecv[k, n * NX : (n + 1) * NX].astype(F32)
            xsend[k] = jnp.where(xl == 0, total[1], total[0]).astype(BF16)
            send(xsend.at[k], xrecv.at[k], x_send, x_recv.at[k], partner)
            sf[k] = jnp.where(xl == 0, total[0], total[1])
        elif step == 2:
            wait_bytes(xrecv.at[k], x_recv.at[k])
            finish(1, k, sf[k] + xrecv[k].astype(F32))

    def reduce_all(g, k, step):
        low, high, _ = GROUPS[g]
        dsend, drecv, d_send, d_recv = direct[g]
        if step == 0:
            dsend[k] = pf[k, :, :, :, low:high].reshape(dsend.shape[1:]).astype(BF16)
            for n, (dx, dy) in enumerate(PEERS):
                to, target = peer(dx, dy)
                send(dsend.at[k, to], drecv.at[k, n], d_send, d_recv.at[k], target)
        elif step == 1:
            wait_bytes(drecv.at[k], d_recv.at[k])
            total = pf[k, y, xl, :, low:high]
            for n in range(len(PEERS)):
                total = total + drecv[k, n].astype(F32)
            finish(g, k, total)

    def reduce(g, k, step):
        if k in REDUCE_AT_ONCE[g]:
            return reduce_all(g, k, step)
        if g == 1 and k in REDUCE_IN_TWO:
            return reduce_two(k, step)
        low, high, first = GROUPS[g]
        sf, xsend, xrecv, x_send, x_recv = groups[g][12:]
        if first == "x":
            block = lambda at: sf[k, at]
            if step == 0:
                xsend[k] = pf[k, :, 1 - xl, :, low:high].astype(BF16)
                send(xsend.at[k], xrecv.at[k], x_send, x_recv.at[k], partner)
            elif step == 1:
                wait_bytes(xrecv.at[k], x_recv.at[k])
                sf[k] = pf[k, :, xl, :, low:high] + xrecv[k].astype(F32)
                start_ring(g, k, sf[k, y2])
            elif step == 2:
                relay(g, k, block)
            else:
                finish(g, k, arrived(g, k, block))
        else:
            block = lambda at: pf[k, at, :, :, low:high]
            if step == 0:
                start_ring(g, k, block(y2))
            elif step == 1:
                relay(g, k, block)
            elif step == 2:
                total = arrived(g, k, block)
                xsend[k] = jnp.where(xl == 0, total[1], total[0]).astype(BF16)
                send(xsend.at[k], xrecv.at[k], x_send, x_recv.at[k], partner)
                sf[k] = jnp.where(xl == 0, total[0], total[1])
            else:
                wait_bytes(xrecv.at[k], x_recv.at[k])
                finish(g, k, sf[k] + xrecv[k].astype(F32))

    def spread(g, at, k):
        pair = g.at[at + (pl.ds(y * NX, NX),)]
        wait_bytes(g.at[at + (0,)], gx_recv.at[k])
        send(pair, pair, h_send, hr_recv.at[k], (xl * NY + y2, j))
        send(pair, pair, gy_send, gr_recv.at[k], y_right)
        send(pair, pair, gy_send, gl_recv.at[k], y_left)

    def spread_done(g, at, k):
        for sem in (gr_recv, gl_recv, hr_recv):
            wait_bytes(g.at[at + (pl.ds(0, NX),)], sem.at[k])

    def peer(dx, dy):
        to_x, to_y = lax.rem(xl + dx, NX), lax.rem(y + dy, NY)
        return to_y * NX + to_x, (to_x * NY + to_y, j)

    def gather_all(g, at, n):
        own = g.at[at + (me,)]
        for dx, dy in PEERS:
            send(own, own, gd_send, gd_recv.at[n], peer(dx, dy)[1])

    def gather_y(k):
        if k in GATHER_IN_TWO:
            spread(ag, (k,), k)
            return
        if k in Y_FIRST:
            wait_bytes(ag.at[k, 0], gr_recv.at[k])
            block = ag.at[k, yl * NX + xl, :, cols[0]]
            send(block, block, h_send, hr_recv.at[k], y_right)
            wait_bytes(ag.at[k, 0], gl_recv.at[k])
            block = ag.at[k, yr * NX + xl, :, cols[1]]
            send(block, block, h_send, hl_recv.at[k], y_left)
            return
        wait_bytes(ag.at[k, 0], gx_recv.at[k])
        pair = ag.at[k, pl.ds(y * NX, NX)]
        send(pair, pair, gy_send, gr_recv.at[k], y_right)
        send(pair, pair, gy_send, gl_recv.at[k], y_left)

    def gather_far(k):
        if k in GATHER_IN_TWO:
            return
        if k in Y_FIRST:
            wait_bytes(ag.at[k, 0, :, cols[0]], hr_recv.at[k])
            wait_bytes(ag.at[k, 0, :, cols[1]], hl_recv.at[k])
            for n in range(NY):
                block = ag.at[k, n * NX + xl]
                send(block, block, gx_send, gx_recv.at[k], partner)
            return
        wait_bytes(ag.at[k, pl.ds(0, NX)], gr_recv.at[k])
        block = ag.at[k, yl * NX]
        send(block, block, h_send, hr_recv.at[k], y_right)
        wait_bytes(ag.at[k, pl.ds(0, NX)], gl_recv.at[k])
        block = ag.at[k, yr * NX + 1]
        send(block, block, h_send, hl_recv.at[k], y_left)

    def gather_done(k):
        if k in GATHER_AT_ONCE:
            wait_bytes(ag.at[k, pl.ds(0, NX * NY - 1)], gd_recv.at[k])
            return
        if k in GATHER_IN_TWO:
            spread_done(ag, (k,), k)
            return
        if k in Y_FIRST:
            wait_bytes(ag.at[k, pl.ds(0, NY)], gx_recv.at[k])
            return
        wait_bytes(ag.at[k, 0], hr_recv.at[k])
        wait_bytes(ag.at[k, 0], hl_recv.at[k])

    def attend():
        query = qkv[:, :, :HEAD].reshape(8 * tile, HEAD)
        key = qkv[:, :, HEAD : 2 * HEAD].reshape(8 * tile, HEAD)
        value = qkv[:, :, 2 * HEAD :].reshape(8 * tile, HEAD)
        query_norm = normalize(query.astype(F32)).astype(BF16)
        key_norm = normalize(key.astype(F32)).astype(BF16)
        scores = lax.dot_general(
            query_norm, key_norm, (((1,), (1,)), ((), ())), preferred_element_type=F32
        )
        scores = scores * (temper[0] * (1.0 / math.sqrt(HEAD)))
        weight = jnp.exp(scores - jnp.max(scores, axis=-1, keepdims=True))
        probs = (weight / jnp.sum(weight, axis=-1, keepdims=True)).astype(BF16)
        mg[me] = jnp.dot(probs, value, preferred_element_type=F32).astype(BF16)
        if 8 in GATHER_AT_ONCE:
            gather_all(mg, (), 8)
        else:
            send(mg.at[me], mg.at[me], gx_send, gx_recv.at[8], partner)

    def project_out(k):
        gather_done(k)
        hidden = ag[k].reshape(8 * tile, depth)
        mixed = mg[:, tile * k : tile * (k + 1), :].reshape(8 * tile, HEAD)
        total = jnp.dot(hidden, w_out[...], preferred_element_type=F32)
        total = total + jnp.dot(mixed, w_at[...], preferred_element_type=F32)
        og[k] = total.reshape(og.shape[1:])
        esend[k] = og[k, 1 - c].astype(BF16)
        send(esend.at[k], erecv.at[k], e_send, e_recv.at[k], sibling)

    def combined(k):
        wait_bytes(erecv.at[k], e_recv.at[k])
        return og[k, c] + erecv[k].astype(F32)

    def reduce_out(k, n):
        span = slice(n * half, (n + 1) * half)
        if k not in summed:
            wait_bytes(erecv.at[k], e_recv.at[k])
            summed.append(k)
        value = og[k, c, :, span] + erecv[k, :, span].astype(F32)
        if k in (2, 6) or (k, n) in ((3, 0), (5, 1)):
            wait_bytes(rrecv.at[k, :, cols[n]], z_recv.at[k, n])
            value = value + rrecv[k, :, span].astype(F32)
        rsend[k, :, span] = value.astype(BF16)
        right = k < 4 or (k == 4 and n == 0)
        to = k - 1 if right else k + 1
        send(
            rsend.at[k, :, cols[n]], rrecv.at[to, :, cols[n]], z_send, z_recv.at[to, n],
            z_right if right else z_left,
        )

    def scatter_out(n, total):
        for q in range(4):
            for s in range(4):
                at = q * tile + s * rows
                fsend[n, q * 4 + s] = total[at : at + rows].astype(BF16)
        slot = i * 2 + xh
        for dx in (2, 1, 3, 0):
            to = lax.rem(x + dx, 4)
            for yy in (0, 1):
                for core in (c, 1 - c):
                    src = (yy * NX + lax.rem(to, 2)) * 4 + (to // 2) * 2 + core
                    target = in_plane(dx, 2 * c + yy, core, n)
                    if n or dx or core is not c:
                        send(fsend.at[n, src], frecv.at[n, slot], f_send, f_recv.at[n], target)
                        continue
                    own = y == 2 * c + yy

                    @pl.when(own)
                    def _():
                        frecv[n, slot] = fsend[n, src]

                    @pl.when(jnp.logical_not(own))
                    def _():
                        send(fsend.at[n, src], frecv.at[n, slot], f_send, f_recv.at[n], target)

    def finish_out(k):
        total = combined(k)
        for n in (0, 1):
            wait_bytes(rrecv.at[k, :, cols[n]], z_recv.at[k, n])
        scatter_out(2 if k == 1 else 1, total + rrecv[k].astype(F32))

    summed = []

    def step(op, n, k):
        if op == "r":
            ring(k, n)
        elif op == "b":
            build(1 if k == 1 else 2, k)
        elif op == "p":
            project(n, k)
        elif op in "qm":
            reduce("qm".index(op), k, n)
        elif op == "y":
            gather_y(k)
        elif op == "f":
            gather_far(k)
        elif op == "w":
            for load in loads[4:] if n else loads[:4]:
                load.wait()
        elif op == "a":
            attend()
        elif op == "g" and 8 in GATHER_AT_ONCE:
            if n:
                wait_bytes(mg.at[pl.ds(0, NX * NY - 1)], gd_recv.at[8])
        elif op == "g":
            (spread_done if n else spread)(mg, (), 8)
        elif op == "o":
            project_out(k)
        elif op == "s" and k in (1, 7):
            finish_out(k)
        elif op == "s":
            reduce_out(k, n)

    for word in SCHEDULE:
        name, k = word.split(".")
        with scope(f"{name}#k={k}"):
            step(name[0], int(name[1:] or 0), int(k))

    with scope("last"):
        scatter_out(0, combined(0))
    with scope("final"):
        mine = c == y // 2

        @pl.when(mine)
        def _():
            wait_bytes(frecv.at[0, pl.ds(0, n_lane - 1)], f_recv.at[0])
            wait_bytes(frecv.at[0, pl.ds(0, n_lane - 1)], f_send)

        @pl.when(jnp.logical_not(mine))
        def _():
            wait_bytes(frecv.at[0], f_recv.at[0])
            wait_bytes(frecv.at[0], f_send)

        for n in (1, 2):
            wait_bytes(frecv.at[n], f_recv.at[n])
            wait_bytes(frecv.at[n], f_send)

    for p in range(NX * NY):
        span = slice(p * depth, (p + 1) * depth)
        total = tokens[:, span].astype(F32)
        for n in range(3):
            total = total + frecv[n, 2 * p].astype(F32) + frecv[n, 2 * p + 1].astype(F32)
        out[:, span] = total.astype(BF16)

    wait_bytes(nrecv.at[0, 0, pl.ds(0, n_lane - 1)], n_send)
    wait_bytes(nrecv.at[0], n_send)
    wait_bytes(nrecv.at[:, 0], m_send)
    wait_bytes(xg.at[pl.ds(0, 5), 0], r_send)
    wait_bytes(xg.at[pl.ds(0, 5), 0], s_send)
    for g, scratch in enumerate(groups):
        once, two = len(REDUCE_AT_ONCE[g]), len(REDUCE_IN_TWO) * g
        asend, _, brs, _, bls, _, a_send, _, _, b_send, _, _, _, xsend, _, x_send, _ = scratch
        for ref, sem in ((asend, a_send), (brs, b_send), (bls, b_send)):
            wait_bytes(ref.at[pl.ds(0, NZ - once - two)], sem)
        wait_bytes(xsend.at[pl.ds(0, NZ - once)], x_send)
        if once:
            wait_bytes(direct[g][1].at[pl.ds(0, once)], direct[g][2])
        if two:
            wait_bytes(direct[g][1].at[pl.ds(0, two), pl.ds(0, 3 * NX)], direct[g][2])
    at_once = [k for k in GATHER_AT_ONCE if k < 8]
    late = len(Y_FIRST)
    n = NZ - len(at_once) - late
    for count, blocks in ((n, (1, 4, 2)), (late, (4, 2, 1))):
        for width, sem in zip(blocks, (gx_send, gy_send, h_send)):
            if count:
                wait_bytes(ag.at[pl.ds(0, count), pl.ds(0, width)], sem)
    if at_once:
        wait_bytes(ag.at[pl.ds(0, len(at_once)), pl.ds(0, NX * NY - 1)], gd_send)
    if 8 in GATHER_AT_ONCE:
        wait_bytes(mg.at[pl.ds(0, NX * NY - 1)], gd_send)
    else:
        for width, sem in zip((1, 4, 2), (gx_send, gy_send, h_send)):
            wait_bytes(mg.at[pl.ds(0, width)], sem)
    wait_bytes(esend, e_send)
    wait_bytes(rsend.at[pl.ds(0, 5)], z_send)


def group_scratch(low, high, first, tile):
    dma = pltpu.SemaphoreType.DMA
    width = high - low
    ring = (NZ, tile, width) if first == "x" else (NZ, NX, tile, width)
    swap = (NZ, NY, tile, width) if first == "x" else (NZ, tile, width)
    return tuple(pltpu.VMEM(ring, BF16) for _ in range(6)) + (
        dma, dma((8,)), dma((8,)), dma, dma((8,)), dma((8,)),
        pltpu.VMEM(swap, F32), pltpu.VMEM(swap, BF16), pltpu.VMEM(swap, BF16), dma, dma((8,)),
    )


def per_device(
    tokens, norm_gain, w_query, w_key, w_value, w_inner, bias_inner, w_attn_out, w_outer, temper
):
    rows, width = tokens.shape
    depth = w_query.shape[0]
    hidden = w_inner.shape[1]
    wide = 3 * HEAD
    tile = 4 * rows
    vmem = pl.BlockSpec(memory_space=pltpu.VMEM)
    smem = pl.BlockSpec(memory_space=pltpu.SMEM)
    hbm = pl.BlockSpec(memory_space=pl.ANY)
    dma = pltpu.SemaphoreType.DMA
    return pl.pallas_call(
        block_kernel,
        out_shape=jax.ShapeDtypeStruct((rows, width), BF16),
        in_specs=[hbm, hbm, hbm, smem] + [hbm] * 6,
        out_specs=vmem,
        scratch_shapes=[
            pltpu.VMEM((rows, width), BF16),
            pltpu.VMEM((1, width), F32),
            pltpu.VMEM((hidden // HEAD, HEAD), F32),
            pltpu.VMEM((depth, wide), BF16),
            pltpu.VMEM((depth, hidden), BF16),
            pltpu.VMEM((HEAD, depth), BF16),
            pltpu.VMEM((hidden, depth), BF16),
            pltpu.VMEM((8, rows, depth), BF16),
            pltpu.VMEM((3, 2, 16, rows, depth), BF16),
            pltpu.VMEM((3, 8 * tile, depth), F32),
            pltpu.VMEM((NZ, 2, 4 * tile, depth), BF16),
            pltpu.VMEM((NZ, NY, NX, tile, wide + hidden), F32),
            tuple(group_scratch(*g, tile) for g in GROUPS),
            tuple(
                (
                    pltpu.VMEM((NZ, NX * NY, tile, high - low), BF16),
                    pltpu.VMEM((NZ, len(PEERS), tile, high - low), BF16),
                    dma, dma((8,)),
                )
                for low, high, _ in GROUPS
            ),
            pltpu.VMEM((NZ, tile, wide), BF16),
            pltpu.VMEM((NZ, NX * NY, tile, hidden), BF16),
            pltpu.VMEM((NX * NY, 8 * tile, HEAD), BF16),
            pltpu.VMEM((NZ, 2, 4 * tile, depth), F32),
            pltpu.VMEM((NZ, 4 * tile, depth), BF16),
            pltpu.VMEM((NZ, 4 * tile, depth), BF16),
            pltpu.VMEM((NZ, 4 * tile, depth), BF16),
            pltpu.VMEM((NZ + 1, 4 * tile, depth), BF16),
            pltpu.VMEM((3, 16, rows, depth), BF16),
            pltpu.VMEM((3, 16, rows, depth), BF16),
            dma((3,)), dma((6,)), dma, dma((3,)), dma, dma((3,)), dma, dma((8, 2)), dma, dma((8,)),
            dma, dma((9,)),
            dma, dma((9,)), dma, dma((9,)), dma((9,)), dma, dma((9,)), dma((9,)),
            dma, dma((8,)), dma, dma((9, 2)), dma, dma((3,)),
        ],
        compiler_params=pltpu.CompilerParams(
            collective_id=0, has_side_effects=True, vmem_limit_bytes=60 * 1024 * 1024
        ),
        name="encoder_block",
    )(
        tokens, norm_gain.reshape(1, -1), bias_inner.reshape(-1, HEAD), temper,
        w_query, w_key, w_value, w_inner, w_attn_out, w_outer,
    )


def solution(mesh):
    return jax.shard_map(
        per_device,
        mesh=mesh,
        in_specs=(
            P(("dp", "mp"), None),
            P(),
            P("dp", "mp"),
            P("dp", "mp"),
            P("dp", "mp"),
            P("dp", "mp"),
            P("mp"),
            P("mp", "dp"),
            P("mp", "dp"),
            P("mp"),
        ),
        out_specs=P(("dp", "mp"), None),
        check_vma=False,
    )
```

time: 117 us -> 76.4 us (0.65)
  Pallas kernels: 114 us -> 74.1 us
  local copies, waits for them, and re-layouts: 2.7 us -> 1.44 us
    pallas_call x1, Pallas kernels: 114 us -> 74.1 us  [per_device(): pl.pallas_call(block_kernel, out_shape=jax.ShapeDtypeStruct((rows, width)...]
    reshape x1 -> x0, local copies, waits for them, and re-layouts: 1.27 us -> none  [per_device(): bias_inner.reshape(1, -1)]
where the time goes in v2:
time: 76.4 us; the launch traced here: 76.2 us
  Pallas kernels  74.1 us (97%)
  local copies, waits for them, and re-layouts  1.44 us (2%)
    pallas_call x1, Pallas kernels, per_device(): pl.pallas_call(block_kernel, out_shape=jax.ShapeDtypeStruct((rows, width)...  74.1 us

profile of v2, /device:TPU:1, one launch (start us, length us, event | category | flops | bytes accessed | tf_op | source)
XLA Modules:
  0.0 76.2 jit_solution(16179495581307466240)
XLA Ops:
  0.7 74.1 %encoder_block.1 = bf16[4,6144]{1,0:T(4,128)(2,1)} custom-call(bf16[4,6144]{1,0:T(4,128)(2,1)} %tokens_ref.1, f32[1,6144]{1,0:T(1,128)} %bitcast.2, f32[6,128]{1,0:T(8,128)} %bitcast.3, f32[1]{0:T(128)S(6)} %copy.12.temper, bf16[768,128]{1,0:T(8,128)(2,1)} %w_query.1, bf16[768,128]{1,0:T(8,128)(2,1)} %w_key.1, bf16[768,128]{1,0:T(8,128)(2,1)} %w_value.1, ...), custom_call_target="tpu_custom_call" | custom-call | tf_op jit(solution)/shard_map/encoder_block/pallas_call | solution.py:583
  74.8 1.4 %copy.13 = bf16[4,6144]{1,0:T(4,128)(2,1)} copy(bf16[4,6144]{1,0:T(4,128)(2,1)} %encoder_block.1) | data formatting | bytes 98304

commit v3 on v2

--- a/solution.py
+++ b/solution.py
@@ -13,26 +13,28 @@
 MESH = pl.DeviceIdType.MESH
 F32, BF16 = jnp.float32, jnp.bfloat16
 GROUPS = ((0, 384, "x"), (384, 1152, "y"))
-REDUCE_AT_ONCE = ((), (5,))
-REDUCE_IN_TWO = (0, 4)
-GATHER_AT_ONCE = (4, 7, 8)
+REDUCE_AT_ONCE = ((4, 6, 7), (4, 5))
+REDUCE_IN_TWO = (0, 3)
+GATHER_AT_ONCE = (4, 7)
 GATHER_IN_TWO = (1,)
 Y_FIRST = (5, 6)
+X_THEN_ALL = ()
+MIX = ((4,), (3, 5), (2, 6), (1, 7), (0,))
+PLACE = {k: n for n, k in enumerate(sum(MIX, ()))}
 PEERS = tuple((dx, dy) for dy in (2, 1, 3, 0) for dx in (1, 0) if dx or dy)
 SCHEDULE = (
-    "r.0", "w0.0", "p0.0", "p1.0", "b.1", "r0.1", "p0.1", "r1.1", "q0.0", "b.7",
-    "r0.7", "p0.7", "m0.0", "q0.7", "r1.7", "p1.1", "r0.2", "q0.1", "m0.1", "r0.6",
-    "q1.0", "p1.7", "r1.2", "m0.7", "q1.7", "r1.6", "p0.2", "p1.2", "q0.2", "m0.2",
-    "m1.0", "p0.6", "m1.1", "p1.6", "m0.6", "q0.6", "r0.3", "r0.5", "q1.1", "q2.7",
-    "q2.0", "r1.3", "r1.5", "m1.2", "p0.3", "q0.3", "p0.5", "q0.5", "p1.5", "q1.2",
-    "m0.5", "q1.6", "r.4", "q3.0", "p1.3", "m0.3", "p0.4", "p1.4", "m0.4", "q0.4",
-    "q1.5", "m2.0", "m2.1", "q1.3", "m1.6", "m1.3", "q1.4", "m2.2", "q2.2", "q2.6",
-    "q3.7", "y.0", "m1.4", "m1.5", "q2.1", "q2.5", "q2.3", "m3.1", "q2.4", "m1.7",
-    "m2.3", "q3.2", "m2.6", "m2.4", "q3.3", "q3.6", "y.5", "q3.4", "m3.3", "q3.1",
-    "q3.5", "m3.2", "m3.6", "a.0", "y.3", "y.6", "m2.7", "f.5", "g0.0", "y.2",
-    "f.3", "g1.0", "w1.0", "o.4", "f.6", "f.0", "s1.4", "s0.4", "f.2", "o.5",
-    "m3.7", "y.1", "o.3", "s0.5", "o.0", "s1.3", "s1.5", "s0.3", "o.6", "o.2",
-    "s0.6", "s1.2", "s1.6", "s0.2", "o.7", "o.1", "s0.7", "s0.1",
+    "r.0", "w0.0", "p0.0", "q0.0", "p1.0", "m0.0", "b.7", "r0.7", "b.1", "r0.1",
+    "p0.1", "q0.1", "p1.1", "r1.7", "p0.7", "r1.1", "m0.1", "q1.0", "q0.7", "p1.7",
+    "m0.7", "r0.6", "r0.2", "q1.1", "m1.0", "r1.6", "q2.0", "r1.2", "m1.1", "p0.6",
+    "p1.6", "m0.6", "q0.6", "m1.7", "q2.1", "p0.2", "q0.2", "r0.5", "p1.2", "m0.2",
+    "r1.5", "r0.3", "q3.0", "r1.3", "m1.6", "p0.3", "q0.3", "p1.3", "p0.5", "m0.3",
+    "q1.7", "q0.5", "q1.2", "p1.5", "m0.5", "r.4", "q1.3", "p0.4", "m2.6", "p1.4",
+    "m2.1", "m0.4", "m1.3", "m1.2", "q1.5", "q0.4", "m2.0", "q2.3", "q1.6", "m3.6",
+    "q2.2", "m1.5", "q3.1", "m2.3", "m2.2", "q2.5", "m1.4", "q1.4", "y.3", "y.5",
+    "q3.3", "y.6", "m3.1", "q3.5", "q3.2", "m3.2", "a.0", "f.3", "y.2", "y.0",
+    "f.5", "y.1", "m2.7", "w1.0", "o.4", "f.6", "s1.4", "s0.4", "o.3", "f.2",
+    "o.5", "m3.7", "s1.3", "s0.5", "s1.5", "s0.3", "o.6", "o.2", "f.0", "s1.2",
+    "s0.6", "s0.2", "s1.6", "o.1", "o.7", "o.0", "s0.1", "s0.7",
 )
 OFFSETS = sorted(
     ((dx, dy) for dx in range(4) for dy in range(NY)),
@@ -189,7 +191,7 @@
     def finish(g, k, total):
         low, high, _ = GROUPS[g]
         if g == 0:
-            qkv[k] = total.astype(BF16)
+            qkv[PLACE[k]] = total.astype(BF16)
             return
         low, high = low - 384, high - 384
         shift = jnp.concatenate([bias[h : h + 1] for h in range(low // HEAD, high // HEAD)], axis=1)
@@ -264,6 +266,26 @@
             wait_bytes(xrecv.at[k], x_recv.at[k])
             finish(1, k, sf[k] + xrecv[k].astype(F32))
 
+    def reduce_x_then_all(k, step):
+        low, high, _ = GROUPS[0]
+        dsend, drecv, d_send, d_recv = direct[0]
+        sf, xsend, xrecv, x_send, x_recv = groups[0][12:]
+        if step == 0:
+            xsend[k] = pf[k, :, 1 - xl, :, low:high].astype(BF16)
+            send(xsend.at[k], xrecv.at[k], x_send, x_recv.at[k], partner)
+        elif step == 1:
+            wait_bytes(xrecv.at[k], x_recv.at[k])
+            sf[k] = pf[k, :, xl, :, low:high] + xrecv[k].astype(F32)
+            dsend[k, :NY] = sf[k].astype(BF16)
+            for n, to in enumerate((y2, yr, yl)):
+                send(dsend.at[k, to], drecv.at[k, n], d_send, d_recv.at[k], (xl * NY + to, j))
+        elif step == 2:
+            wait_bytes(drecv.at[k, pl.ds(0, 3)], d_recv.at[k])
+            total = sf[k, y]
+            for n in range(3):
+                total = total + drecv[k, n].astype(F32)
+            finish(0, k, total)
+
     def reduce_all(g, k, step):
         low, high, _ = GROUPS[g]
         dsend, drecv, d_send, d_recv = direct[g]
@@ -282,6 +304,8 @@
     def reduce(g, k, step):
         if k in REDUCE_AT_ONCE[g]:
             return reduce_all(g, k, step)
+        if g == 0 and k in X_THEN_ALL:
+            return reduce_x_then_all(k, step)
         if g == 1 and k in REDUCE_IN_TWO:
             return reduce_two(k, step)
         low, high, first = GROUPS[g]
@@ -394,15 +418,25 @@
         weight = jnp.exp(scores - jnp.max(scores, axis=-1, keepdims=True))
         probs = (weight / jnp.sum(weight, axis=-1, keepdims=True)).astype(BF16)
         mg[me] = jnp.dot(probs, value, preferred_element_type=F32).astype(BF16)
-        if 8 in GATHER_AT_ONCE:
-            gather_all(mg, (), 8)
-        else:
-            send(mg.at[me], mg.at[me], gx_send, gx_recv.at[8], partner)
+        for n, group in enumerate(MIX):
+            own = mg.at[me, pl.ds(PLACE[group[0]] * tile, len(group) * tile)]
+            for dx, dy in PEERS:
+                send(own, own, gd_send, gd_recv.at[8 + n], peer(dx, dy)[1])
+
+    mixed_here = []
+
+    def mixed_done(k):
+        for n, group in enumerate(MIX):
+            if k in group and n not in mixed_here:
+                wait_bytes(mg.at[pl.ds(0, len(PEERS)), pl.ds(0, len(group) * tile)], gd_recv.at[8 + n])
+                mixed_here.append(n)
 
     def project_out(k):
         gather_done(k)
+        mixed_done(k)
         hidden = ag[k].reshape(8 * tile, depth)
-        mixed = mg[:, tile * k : tile * (k + 1), :].reshape(8 * tile, HEAD)
+        at = tile * PLACE[k]
+        mixed = mg[:, at : at + tile, :].reshape(8 * tile, HEAD)
         total = jnp.dot(hidden, w_out[...], preferred_element_type=F32)
         total = total + jnp.dot(mixed, w_at[...], preferred_element_type=F32)
         og[k] = total.reshape(og.shape[1:])
@@ -481,11 +515,6 @@
                 load.wait()
         elif op == "a":
             attend()
-        elif op == "g" and 8 in GATHER_AT_ONCE:
-            if n:
-                wait_bytes(mg.at[pl.ds(0, NX * NY - 1)], gd_recv.at[8])
-        elif op == "g":
-            (spread_done if n else spread)(mg, (), 8)
         elif op == "o":
             project_out(k)
         elif op == "s" and k in (1, 7):
@@ -530,7 +559,7 @@
     wait_bytes(xg.at[pl.ds(0, 5), 0], r_send)
     wait_bytes(xg.at[pl.ds(0, 5), 0], s_send)
     for g, scratch in enumerate(groups):
-        once, two = len(REDUCE_AT_ONCE[g]), len(REDUCE_IN_TWO) * g
+        once, two = len(REDUCE_AT_ONCE[g]), len((X_THEN_ALL, REDUCE_IN_TWO)[g])
         asend, _, brs, _, bls, _, a_send, _, _, b_send, _, _, _, xsend, _, x_send, _ = scratch
         for ref, sem in ((asend, a_send), (brs, b_send), (bls, b_send)):
             wait_bytes(ref.at[pl.ds(0, NZ - once - two)], sem)
@@ -538,7 +567,7 @@
         if once:
             wait_bytes(direct[g][1].at[pl.ds(0, once)], direct[g][2])
         if two:
-            wait_bytes(direct[g][1].at[pl.ds(0, two), pl.ds(0, 3 * NX)], direct[g][2])
+            wait_bytes(direct[g][1].at[pl.ds(0, two), pl.ds(0, 3 + 3 * g)], direct[g][2])
     at_once = [k for k in GATHER_AT_ONCE if k < 8]
     late = len(Y_FIRST)
     n = NZ - len(at_once) - late
@@ -548,11 +577,7 @@
                 wait_bytes(ag.at[pl.ds(0, count), pl.ds(0, width)], sem)
     if at_once:
         wait_bytes(ag.at[pl.ds(0, len(at_once)), pl.ds(0, NX * NY - 1)], gd_send)
-    if 8 in GATHER_AT_ONCE:
-        wait_bytes(mg.at[pl.ds(0, NX * NY - 1)], gd_send)
-    else:
-        for width, sem in zip((1, 4, 2), (gx_send, gy_send, h_send)):
-            wait_bytes(mg.at[pl.ds(0, width)], sem)
+    wait_bytes(mg.at[pl.ds(0, NX * NY - 1)], gd_send)
     wait_bytes(esend, e_send)
     wait_bytes(rsend.at[pl.ds(0, 5)], z_send)
 
@@ -618,7 +643,7 @@
             pltpu.VMEM((3, 16, rows, depth), BF16),
             pltpu.VMEM((3, 16, rows, depth), BF16),
             dma((3,)), dma((6,)), dma, dma((3,)), dma, dma((3,)), dma, dma((8, 2)), dma, dma((8,)),
-            dma, dma((9,)),
+            dma, dma((13,)),
             dma, dma((9,)), dma, dma((9,)), dma((9,)), dma, dma((9,)), dma((9,)),
             dma, dma((8,)), dma, dma((9, 2)), dma, dma((3,)),
         ],

time: 76.4 us -> 75.6 us (0.990)
  no operation moved by 1% of the time
where the time goes in v3:
time: 75.6 us; the launch traced here: 75.5 us
  Pallas kernels  73.4 us (97%)
  local copies, waits for them, and re-layouts  1.44 us (2%)
    pallas_call x1, Pallas kernels, per_device(): pl.pallas_call(block_kernel, out_shape=jax.ShapeDtypeStruct((rows, width)...  73.4 us

profile of v3, /device:TPU:1, one launch (start us, length us, event | category | flops | bytes accessed | tf_op | source)
XLA Modules:
  0.0 75.5 jit_solution(15097568226299411411)
XLA Ops:
  0.7 73.4 %encoder_block.1 = bf16[4,6144]{1,0:T(4,128)(2,1)} custom-call(bf16[4,6144]{1,0:T(4,128)(2,1)} %tokens_ref.1, f32[1,6144]{1,0:T(1,128)} %bitcast.2, f32[6,128]{1,0:T(8,128)} %bitcast.3, f32[1]{0:T(128)S(6)} %copy.12.temper, bf16[768,128]{1,0:T(8,128)(2,1)} %w_query.1, bf16[768,128]{1,0:T(8,128)(2,1)} %w_key.1, bf16[768,128]{1,0:T(8,128)(2,1)} %w_value.1, ...), custom_call_target="tpu_custom_call" | custom-call | tf_op jit(solution)/shard_map/encoder_block/pallas_call | solution.py:608
  74.0 1.4 %copy.13 = bf16[4,6144]{1,0:T(4,128)(2,1)} copy(bf16[4,6144]{1,0:T(4,128)(2,1)} %encoder_block.1) | data formatting | bytes 98304

commit v4 on v3

--- a/solution.py
+++ b/solution.py
@@ -13,28 +13,29 @@
 MESH = pl.DeviceIdType.MESH
 F32, BF16 = jnp.float32, jnp.bfloat16
 GROUPS = ((0, 384, "x"), (384, 1152, "y"))
-REDUCE_AT_ONCE = ((4, 6, 7), (4, 5))
-REDUCE_IN_TWO = (0, 3)
-GATHER_AT_ONCE = (4, 7)
-GATHER_IN_TWO = (1,)
-Y_FIRST = (5, 6)
-X_THEN_ALL = ()
+REDUCE_AT_ONCE = ((1,), (4, 5))
+REDUCE_IN_TWO = ()
+GATHER_AT_ONCE = (4,)
+GATHER_IN_TWO = (1, 2, 3)
+Y_FIRST = (5, 6, 7)
+X_THEN_ALL = (2,)
 MIX = ((4,), (3, 5), (2, 6), (1, 7), (0,))
 PLACE = {k: n for n, k in enumerate(sum(MIX, ()))}
 PEERS = tuple((dx, dy) for dy in (2, 1, 3, 0) for dx in (1, 0) if dx or dy)
 SCHEDULE = (
-    "r.0", "w0.0", "p0.0", "q0.0", "p1.0", "m0.0", "b.7", "r0.7", "b.1", "r0.1",
-    "p0.1", "q0.1", "p1.1", "r1.7", "p0.7", "r1.1", "m0.1", "q1.0", "q0.7", "p1.7",
-    "m0.7", "r0.6", "r0.2", "q1.1", "m1.0", "r1.6", "q2.0", "r1.2", "m1.1", "p0.6",
-    "p1.6", "m0.6", "q0.6", "m1.7", "q2.1", "p0.2", "q0.2", "r0.5", "p1.2", "m0.2",
-    "r1.5", "r0.3", "q3.0", "r1.3", "m1.6", "p0.3", "q0.3", "p1.3", "p0.5", "m0.3",
-    "q1.7", "q0.5", "q1.2", "p1.5", "m0.5", "r.4", "q1.3", "p0.4", "m2.6", "p1.4",
-    "m2.1", "m0.4", "m1.3", "m1.2", "q1.5", "q0.4", "m2.0", "q2.3", "q1.6", "m3.6",
-    "q2.2", "m1.5", "q3.1", "m2.3", "m2.2", "q2.5", "m1.4", "q1.4", "y.3", "y.5",
-    "q3.3", "y.6", "m3.1", "q3.5", "q3.2", "m3.2", "a.0", "f.3", "y.2", "y.0",
-    "f.5", "y.1", "m2.7", "w1.0", "o.4", "f.6", "s1.4", "s0.4", "o.3", "f.2",
-    "o.5", "m3.7", "s1.3", "s0.5", "s1.5", "s0.3", "o.6", "o.2", "f.0", "s1.2",
-    "s0.6", "s0.2", "s1.6", "o.1", "o.7", "o.0", "s0.1", "s0.7",
+    "r.0", "w0.0", "p0.0", "p1.0", "q0.0", "b.1", "r0.1", "r1.1", "m0.0", "b.7",
+    "p0.7", "r0.7", "p0.1", "p1.1", "p1.7", "m0.7", "r1.7", "q0.1", "m0.1", "q0.7",
+    "m1.0", "r0.2", "q1.0", "r0.6", "r1.2", "m1.7", "r1.6", "p0.2", "p1.2", "m0.2",
+    "p0.6", "q0.6", "m1.1", "q1.7", "m2.0", "p1.6", "q0.2", "q2.0", "r0.5", "r0.3",
+    "q1.1", "r1.3", "r1.5", "m0.6", "p0.3", "m1.2", "q0.3", "p0.5", "p1.5", "q1.6",
+    "m0.5", "q3.0", "r.4", "q0.5", "p1.3", "m0.3", "p0.4", "q1.3", "m2.7", "m1.6",
+    "q0.4", "p1.4", "m0.4", "m1.3", "q1.5", "m2.2", "q1.2", "q1.4", "m3.0", "q2.7",
+    "m2.1", "m2.6", "m3.7", "m1.5", "q2.3", "q2.6", "m2.3", "q2.5", "q2.4", "m1.4",
+    "q2.2", "m3.3", "q3.7", "q3.6", "y.5", "q3.3", "y.7", "m3.2", "q3.5", "m3.6",
+    "q3.4", "a.0", "f.5", "y.6", "m3.1", "y.3", "y.0", "w1.0", "o.4", "f.6",
+    "y.2", "s1.4", "s0.4", "o.5", "o.3", "f.0", "s0.5", "s0.3", "s1.5", "y.1",
+    "s1.3", "o.6", "f.7", "o.2", "s0.6", "o.0", "s0.2", "s1.6", "s1.2", "o.1",
+    "o.7", "s0.7", "s0.1",
 )
 OFFSETS = sorted(
     ((dx, dy) for dx in range(4) for dy in range(NY)),

time: 75.6 us -> 74.5 us (0.985)
  Pallas kernels: 73.4 us -> 72.3 us
    pallas_call x1, Pallas kernels: 73.4 us -> 72.3 us  [per_device(): pl.pallas_call(block_kernel, out_shape=jax.ShapeDtypeStruct((rows, width)...]
where the time goes in v4:
time: 74.5 us; the launch traced here: 74.4 us
  Pallas kernels  72.3 us (97%)
  local copies, waits for them, and re-layouts  1.44 us (2%)
    pallas_call x1, Pallas kernels, per_device(): pl.pallas_call(block_kernel, out_shape=jax.ShapeDtypeStruct((rows, width)...  72.3 us

profile of v4, /device:TPU:1, one launch (start us, length us, event | category | flops | bytes accessed | tf_op | source)
XLA Modules:
  0.0 74.4 jit_solution(13599250303786861834)
XLA Ops:
  0.7 72.3 %encoder_block.1 = bf16[4,6144]{1,0:T(4,128)(2,1)} custom-call(bf16[4,6144]{1,0:T(4,128)(2,1)} %tokens_ref.1, f32[1,6144]{1,0:T(1,128)} %bitcast.2, f32[6,128]{1,0:T(8,128)} %bitcast.3, f32[1]{0:T(128)S(6)} %copy.12.temper, bf16[768,128]{1,0:T(8,128)(2,1)} %w_query.1, bf16[768,128]{1,0:T(8,128)(2,1)} %w_key.1, bf16[768,128]{1,0:T(8,128)(2,1)} %w_value.1, ...), custom_call_target="tpu_custom_call" | custom-call | tf_op jit(solution)/shard_map/encoder_block/pallas_call | solution.py:609
  72.9 1.4 %copy.13 = bf16[4,6144]{1,0:T(4,128)(2,1)} copy(bf16[4,6144]{1,0:T(4,128)(2,1)} %encoder_block.1) | data formatting | bytes 98304

commit v5 on v3

--- a/solution.py
+++ b/solution.py
@@ -13,28 +13,29 @@
 MESH = pl.DeviceIdType.MESH
 F32, BF16 = jnp.float32, jnp.bfloat16
 GROUPS = ((0, 384, "x"), (384, 1152, "y"))
-REDUCE_AT_ONCE = ((4, 6, 7), (4, 5))
-REDUCE_IN_TWO = (0, 3)
+REDUCE_AT_ONCE = ((1,), (4, 5))
+REDUCE_IN_TWO = (0,)
 GATHER_AT_ONCE = (4, 7)
-GATHER_IN_TWO = (1,)
-Y_FIRST = (5, 6)
-X_THEN_ALL = ()
+GATHER_IN_TWO = (2, 3)
+Y_FIRST = (1, 5, 6)
+X_THEN_ALL = (2, 3, 4)
 MIX = ((4,), (3, 5), (2, 6), (1, 7), (0,))
 PLACE = {k: n for n, k in enumerate(sum(MIX, ()))}
 PEERS = tuple((dx, dy) for dy in (2, 1, 3, 0) for dx in (1, 0) if dx or dy)
 SCHEDULE = (
-    "r.0", "w0.0", "p0.0", "q0.0", "p1.0", "m0.0", "b.7", "r0.7", "b.1", "r0.1",
-    "p0.1", "q0.1", "p1.1", "r1.7", "p0.7", "r1.1", "m0.1", "q1.0", "q0.7", "p1.7",
-    "m0.7", "r0.6", "r0.2", "q1.1", "m1.0", "r1.6", "q2.0", "r1.2", "m1.1", "p0.6",
-    "p1.6", "m0.6", "q0.6", "m1.7", "q2.1", "p0.2", "q0.2", "r0.5", "p1.2", "m0.2",
-    "r1.5", "r0.3", "q3.0", "r1.3", "m1.6", "p0.3", "q0.3", "p1.3", "p0.5", "m0.3",
-    "q1.7", "q0.5", "q1.2", "p1.5", "m0.5", "r.4", "q1.3", "p0.4", "m2.6", "p1.4",
-    "m2.1", "m0.4", "m1.3", "m1.2", "q1.5", "q0.4", "m2.0", "q2.3", "q1.6", "m3.6",
-    "q2.2", "m1.5", "q3.1", "m2.3", "m2.2", "q2.5", "m1.4", "q1.4", "y.3", "y.5",
-    "q3.3", "y.6", "m3.1", "q3.5", "q3.2", "m3.2", "a.0", "f.3", "y.2", "y.0",
-    "f.5", "y.1", "m2.7", "w1.0", "o.4", "f.6", "s1.4", "s0.4", "o.3", "f.2",
-    "o.5", "m3.7", "s1.3", "s0.5", "s1.5", "s0.3", "o.6", "o.2", "f.0", "s1.2",
-    "s0.6", "s0.2", "s1.6", "o.1", "o.7", "o.0", "s0.1", "s0.7",
+    "r.0", "w0.0", "p0.0", "b.1", "q0.0", "r0.1", "b.7", "r0.7", "p0.1", "p1.0",
+    "r1.7", "q0.1", "r1.1", "p0.7", "p1.7", "m0.0", "p1.1", "q0.7", "r0.6", "m0.1",
+    "q1.0", "r0.2", "r1.6", "m0.7", "r1.2", "p0.6", "p1.6", "m0.6", "p0.2", "m1.1",
+    "q0.2", "q1.7", "r0.3", "p1.2", "m0.2", "q2.0", "m1.0", "q0.6", "r0.5", "r1.5",
+    "r1.3", "m1.6", "p0.5", "p0.3", "q0.5", "p1.3", "m0.3", "q0.3", "p1.5", "m0.5",
+    "r.4", "q1.2", "p0.4", "q1.6", "m1.3", "q1.1", "q1.5", "p1.4", "q0.4", "m0.4",
+    "q2.2", "m1.2", "m2.6", "q2.5", "m2.3", "q1.3", "m1.5", "m2.1", "q2.6", "q1.4",
+    "q2.7", "m1.7", "m2.0", "m2.2", "q3.0", "m3.6", "m3.3", "y.5", "q2.3", "m1.4",
+    "q3.7", "q2.4", "q3.5", "q3.6", "a.0", "h0.4", "m3.1", "y.6", "m2.7", "m3.2",
+    "h1.4", "y.3", "f.5", "h2.4", "y.0", "y.2", "w1.0", "o.4", "f.6", "s1.4",
+    "s0.4", "h4.4", "y.1", "o.5", "h3.4", "o.3", "s0.5", "m3.7", "s1.3", "s1.5",
+    "s0.3", "o.6", "f.1", "o.2", "s0.6", "f.0", "s1.2", "s1.6", "s0.2", "o.7",
+    "o.1", "o.0", "s0.7", "s0.1",
 )
 OFFSETS = sorted(
     ((dx, dy) for dx in range(4) for dy in range(NY)),
@@ -418,10 +419,11 @@
         weight = jnp.exp(scores - jnp.max(scores, axis=-1, keepdims=True))
         probs = (weight / jnp.sum(weight, axis=-1, keepdims=True)).astype(BF16)
         mg[me] = jnp.dot(probs, value, preferred_element_type=F32).astype(BF16)
-        for n, group in enumerate(MIX):
-            own = mg.at[me, pl.ds(PLACE[group[0]] * tile, len(group) * tile)]
-            for dx, dy in PEERS:
-                send(own, own, gd_send, gd_recv.at[8 + n], peer(dx, dy)[1])
+
+    def gather_mixed(n):
+        own = mg.at[me, pl.ds(PLACE[MIX[n][0]] * tile, len(MIX[n]) * tile)]
+        for dx, dy in PEERS:
+            send(own, own, gd_send, gd_recv.at[8 + n], peer(dx, dy)[1])
 
     mixed_here = []
 
@@ -515,6 +517,8 @@
                 load.wait()
         elif op == "a":
             attend()
+        elif op == "h":
+            gather_mixed(n)
         elif op == "o":
             project_out(k)
         elif op == "s" and k in (1, 7):
@@ -607,7 +611,7 @@
     dma = pltpu.SemaphoreType.DMA
     return pl.pallas_call(
         block_kernel,
-        out_shape=jax.ShapeDtypeStruct((rows, width), BF16),
+        out_shape=pltpu.VMEM((rows, width), BF16),
         in_specs=[hbm, hbm, hbm, smem] + [hbm] * 6,
         out_specs=vmem,
         scratch_shapes=[

time: 75.6 us -> 72.6 us (0.960)
  Pallas kernels: 73.4 us -> 71.3 us
  local copies, waits for them, and re-layouts: 1.44 us -> 0.62 us
    pallas_call x1, Pallas kernels: 73.4 us -> 71.3 us  [per_device(): pl.pallas_call(block_kernel, out_shape=pltpu.VMEM((rows, width), BF16), i...]
    unnamed x1, local copies, waits for them, and re-layouts: 1.44 us -> 0.62 us
where the time goes in v5:
time: 72.6 us; the launch traced here: 72.5 us
  Pallas kernels  71.3 us (98%)
    pallas_call x1, Pallas kernels, per_device(): pl.pallas_call(block_kernel, out_shape=pltpu.VMEM((rows, width), BF16), i...  71.3 us

profile of v5, /device:TPU:1, one launch (start us, length us, event | category | flops | bytes accessed | tf_op | source)
XLA Modules:
  0.0 72.5 jit_solution(12575381819605406988)
XLA Ops:
  0.7 71.3 %encoder_block.1 = bf16[4,6144]{1,0:T(4,128)(2,1)S(1)} custom-call(bf16[4,6144]{1,0:T(4,128)(2,1)} %tokens_ref.1, f32[1,6144]{1,0:T(1,128)} %bitcast.2, f32[6,128]{1,0:T(8,128)} %bitcast.3, f32[1]{0:T(128)S(6)} %copy.13.temper, bf16[768,128]{1,0:T(8,128)(2,1)} %w_query.1, bf16[768,128]{1,0:T(8,128)(2,1)} %w_key.1, bf16[768,128]{1,0:T(8,128)(2,1)} %w_value.1, ...), custom_call_target="tpu_custom_call" | custom-call | tf_op jit(solution)/shard_map/encoder_block/pallas_call | solution.py:612
  71.9 0.6 copy.12

commit v6 on v5

--- a/solution.py
+++ b/solution.py
@@ -13,29 +13,29 @@
 MESH = pl.DeviceIdType.MESH
 F32, BF16 = jnp.float32, jnp.bfloat16
 GROUPS = ((0, 384, "x"), (384, 1152, "y"))
-REDUCE_AT_ONCE = ((1,), (4, 5))
-REDUCE_IN_TWO = (0,)
-GATHER_AT_ONCE = (4, 7)
+REDUCE_AT_ONCE = ((1,), (4, 5, 7))
+REDUCE_IN_TWO = (0, 2)
+GATHER_AT_ONCE = (4,)
 GATHER_IN_TWO = (2, 3)
-Y_FIRST = (1, 5, 6)
+Y_FIRST = (1, 6)
 X_THEN_ALL = (2, 3, 4)
 MIX = ((4,), (3, 5), (2, 6), (1, 7), (0,))
 PLACE = {k: n for n, k in enumerate(sum(MIX, ()))}
 PEERS = tuple((dx, dy) for dy in (2, 1, 3, 0) for dx in (1, 0) if dx or dy)
 SCHEDULE = (
-    "r.0", "w0.0", "p0.0", "b.1", "q0.0", "r0.1", "b.7", "r0.7", "p0.1", "p1.0",
-    "r1.7", "q0.1", "r1.1", "p0.7", "p1.7", "m0.0", "p1.1", "q0.7", "r0.6", "m0.1",
-    "q1.0", "r0.2", "r1.6", "m0.7", "r1.2", "p0.6", "p1.6", "m0.6", "p0.2", "m1.1",
-    "q0.2", "q1.7", "r0.3", "p1.2", "m0.2", "q2.0", "m1.0", "q0.6", "r0.5", "r1.5",
-    "r1.3", "m1.6", "p0.5", "p0.3", "q0.5", "p1.3", "m0.3", "q0.3", "p1.5", "m0.5",
-    "r.4", "q1.2", "p0.4", "q1.6", "m1.3", "q1.1", "q1.5", "p1.4", "q0.4", "m0.4",
-    "q2.2", "m1.2", "m2.6", "q2.5", "m2.3", "q1.3", "m1.5", "m2.1", "q2.6", "q1.4",
-    "q2.7", "m1.7", "m2.0", "m2.2", "q3.0", "m3.6", "m3.3", "y.5", "q2.3", "m1.4",
-    "q3.7", "q2.4", "q3.5", "q3.6", "a.0", "h0.4", "m3.1", "y.6", "m2.7", "m3.2",
-    "h1.4", "y.3", "f.5", "h2.4", "y.0", "y.2", "w1.0", "o.4", "f.6", "s1.4",
-    "s0.4", "h4.4", "y.1", "o.5", "h3.4", "o.3", "s0.5", "m3.7", "s1.3", "s1.5",
-    "s0.3", "o.6", "f.1", "o.2", "s0.6", "f.0", "s1.2", "s1.6", "s0.2", "o.7",
-    "o.1", "o.0", "s0.7", "s0.1",
+    "r.0", "w0.0", "b.1", "r0.1", "b.7", "r0.7", "r1.1", "p0.1", "q0.1", "r1.7",
+    "p0.0", "p1.1", "p1.0", "m0.1", "p0.7", "m0.0", "p1.7", "q0.7", "r0.2", "r0.6",
+    "m0.7", "q0.0", "r1.2", "r1.6", "m1.1", "p0.2", "p1.2", "m0.2", "q1.7", "q0.2",
+    "p0.6", "p1.6", "r0.3", "r0.5", "m0.6", "r1.3", "q0.6", "r1.5", "p0.3", "p0.5",
+    "q0.5", "p1.3", "m0.3", "p1.5", "q1.0", "m0.5", "r.4", "q0.3", "m1.6", "p0.4",
+    "p1.4", "q1.5", "q0.4", "m0.4", "m1.3", "m2.6", "q1.6", "q2.0", "q1.1", "m1.5",
+    "q1.4", "q2.7", "q2.5", "m1.0", "m2.1", "q1.3", "q1.2", "m2.3", "q2.6", "m1.2",
+    "m3.6", "y.5", "m1.4", "q2.4", "q3.7", "q3.0", "q3.6", "q3.5", "q2.2", "q2.3",
+    "m3.3", "a.0", "h0.4", "m2.2", "m1.7", "m3.1", "h1.4", "y.6", "m2.0", "f.5",
+    "y.3", "y.1", "h2.4", "w1.0", "o.4", "y.2", "f.6", "h3.4", "s1.4", "s0.4",
+    "y.7", "y.0", "o.5", "o.3", "s0.5", "s1.3", "h4.4", "s1.5", "s0.3", "o.6",
+    "f.1", "o.2", "f.7", "s0.6", "s1.2", "s1.6", "f.0", "s0.2", "o.7", "o.1",
+    "o.0", "s0.7", "s0.1",
 )
 OFFSETS = sorted(
     ((dx, dy) for dx in range(4) for dy in range(NY)),

time: 72.6 us -> 71.9 us (level)
  Pallas kernels: 71.3 us -> 70.5 us
where the time goes in v6:
time: 71.9 us; the launch traced here: 71.8 us
  Pallas kernels  70.5 us (98%)
    pallas_call x1, Pallas kernels, per_device(): pl.pallas_call(block_kernel, out_shape=pltpu.VMEM((rows, width), BF16), i...  70.5 us

profile of v6, /device:TPU:1, one launch (start us, length us, event | category | flops | bytes accessed | tf_op | source)
XLA Modules:
  0.0 71.8 jit_solution(1901025353730786702)
XLA Ops:
  0.7 70.5 %encoder_block.1 = bf16[4,6144]{1,0:T(4,128)(2,1)S(1)} custom-call(bf16[4,6144]{1,0:T(4,128)(2,1)} %tokens_ref.1, f32[1,6144]{1,0:T(1,128)} %bitcast.2, f32[6,128]{1,0:T(8,128)} %bitcast.3, f32[1]{0:T(128)S(6)} %copy.13.temper, bf16[768,128]{1,0:T(8,128)(2,1)} %w_query.1, bf16[768,128]{1,0:T(8,128)(2,1)} %w_key.1, bf16[768,128]{1,0:T(8,128)(2,1)} %w_value.1, ...), custom_call_target="tpu_custom_call" | custom-call | tf_op jit(solution)/shard_map/encoder_block/pallas_call | solution.py:612
  71.2 0.6 copy.12
